TPU v7x, 16 devices: a 4x2x1 block of a 4x4x8 slice. The times are simulated.
16 devices in a mesh: dp: 2 (over y, z), sp: 8 (over x, core).
Axes of the slice: x: 4, y: 2, z: 1, core: 2. Of those that a mesh axis runs over, the one named last changes fastest.
The devices are a block of a 4x4x8 slice.
Arguments:
- x_in: bfloat16 [4, 8192, 768], P('dp', 'sp'), parts along dimension 0
- grad_y: bfloat16 [4, 8192, 768], P('dp', 'sp'), parts along dimension 0
- ln_gain: float32 [768], replicated
- ln_bias: float32 [768], replicated
- w_qkv: bfloat16 [768, 2304], replicated
- w_out: bfloat16 [768, 768], replicated
- temp_tau: float32 [16], replicated
Outputs:
- output 1: bfloat16 [4, 8192, 768], P('dp', 'sp'), parts along dimension 0
- output 2: bfloat16 [4, 8192, 768], P('dp', 'sp'), parts along dimension 0
- output 3: bfloat16 [1536, 2304], P(('dp', 'sp')), parts along dimension 0
- output 4: bfloat16 [1536, 768], P(('dp', 'sp')), parts along dimension 0
- output 5: float32 [1536], P('dp'), parts along dimension 0
- output 6: float32 [1536], P('dp'), parts along dimension 0
- output 7: float32 [32], P('dp'), parts along dimension 0
There are 2 independent parts. A program takes and returns all parts, laid end to end along the dimension named above; an argument that names none is the same for every part.
All inputs are finite; a program needn't handle non-finite values.
Results may differ from a plain program's by a relative error of at most 0.00885654.
Values are sent between devices in bfloat16 or wider.
A program may use at most 768 MiB of HBM per device.

v0:
```python
import functools

import jax
import jax.numpy as jnp
from jax import lax
from jax.experimental import pallas as pl
from jax.experimental.pallas import tpu as pltpu
from jax.sharding import PartitionSpec as P

LN_EPS = 1e-6
F32 = jnp.float32
BF16 = jnp.bfloat16
LANES = 128
TOK = 512
COLS = 256
NN = (((1,), (0,)), ((), ()))
NT = (((1,), (1,)), ((), ()))


def mm(a, b, dims=NN):
    return lax.dot_general(a, b, dims, preferred_element_type=F32)


def xca_kernel(
    n, heads,
    x_hbm, dy_hbm, gain_ref, bias_ref, wqkv_hbm, wo_hbm, tau_ref,
    y_hbm, dx_hbm, dwqkv_ref, dwo_ref, dgain_ref, dbias_ref, dtau_ref,
    x_v, dy_v, w_v, wt_v, wo_v, ut, zt, dot_v, ot, y_st,
    sq_acc, gs_out, gs_in, gs_sum, a_all, ds_out, ds_in, g_all, c_all, bd, colq, colk, dgb, gb_out, gb_all,
    part, r1, r2, r3,
    in_sem, out_sem, d2d_s, d2d_r, p1_s, p1_r, p2_s, p2_r,
    gs_s, gs_r, a_s, a_r, ds_s, ds_r, g_s, g_r, c_s, c_r, gb_s, gb_r,
):
    images, tokens, dim = x_hbm.shape
    hd = dim // heads
    rows = images * tokens
    per_dev = dim // n
    chips = n // 2
    wheads = COLS // hd
    wrow = wheads * hd
    nwin = -(-heads // wheads)
    tiles = tokens // TOK
    o_chunks = dim // COLS
    chunks = 4 * o_chunks
    me = lax.axis_index("sp")
    chip, core = me // 2, me % 2
    right = ((chip + 1) % chips) * 2 + core
    left = ((chip + chips - 1) % chips) * 2 + core
    partner = chip * 2 + (1 - core)
    cr, cl, co = (chip + 1) % chips, (chip + chips - 1) % chips, (chip + 2) % chips

    def rcopy(src, dst, ss, rs, dev):
        return pltpu.make_async_remote_copy(
            src_ref=src, dst_ref=dst, send_sem=ss, recv_sem=rs,
            device_id={"sp": dev}, device_id_type=pl.DeviceIdType.MESH)

    def cp_x(b):
        return pltpu.make_async_copy(x_hbm.at[b], x_v.at[pl.ds(b * tokens, tokens)], in_sem.at[b])

    def cp_dy(b):
        return pltpu.make_async_copy(dy_hbm.at[b], dy_v.at[pl.ds(b * tokens, tokens)], in_sem.at[2 + b])

    cp_w = pltpu.make_async_copy(wqkv_hbm, w_v, in_sem.at[4])
    cp_wo = pltpu.make_async_copy(wo_hbm, wo_v, in_sem.at[5])
    cp_w.start()
    cp_x(0).start()
    cp_x(1).start()
    cp_wo.start()
    cp_dy(0).start()
    cp_dy(1).start()

    barrier = pltpu.get_barrier_semaphore()
    for k in range(1, n):
        pl.semaphore_signal(barrier, inc=1, device_id={"sp": (me + k) % n},
                            device_id_type=pl.DeviceIdType.MESH)

    sq_acc[...] = jnp.zeros_like(sq_acc)
    bd[...] = jnp.zeros_like(bd)
    dgb[...] = jnp.zeros_like(dgb)

    cp_w.wait()

    def wt_body(i, _):
        off = pl.multiple_of(i * COLS, COLS)
        wt_v[pl.ds(off, COLS), :] = w_v[:, pl.ds(off, COLS)].T
        return 0
    lax.fori_loop(0, 3 * dim // COLS, wt_body, 0)

    def norm(xt):
        mean = jnp.sum(xt, axis=-1, keepdims=True) * (1.0 / dim)
        cen = xt - mean
        inv = lax.rsqrt(jnp.sum(cen * cen, axis=-1, keepdims=True) * (1.0 / dim) + LN_EPS)
        return cen * inv, inv

    gain_row = gain_ref[...]
    bias_row = bias_ref[...]

    lane_w = lax.broadcasted_iota(jnp.int32, (hd, LANES), 1)

    def to_pairs(blocks, out_ref):
        for d in range(n):
            picked = []
            for s in range(2):
                w, k = divmod(2 * d + s, wheads)
                strip = blocks[w][k * hd:(k + 1) * hd, :]
                shift = (s * hd - k * hd) % COLS
                if shift:
                    strip = pltpu.roll(strip, shift, 1)
                picked.append(strip[:, :LANES])
            out_ref[d, 0:hd, :] = jnp.where(lane_w < hd, picked[0], jnp.where(lane_w < 2 * hd, picked[1], 0.0))

    def gram(b, l_ref, l0, r_ref, r0):
        blocks = []
        for w in range(nwin):
            m = min(wrow, dim - w * wrow)
            lo, ro = l0 + w * wrow, r0 + w * wrow
            nw = min(COLS, dim - w * wrow)
            left_op = l_ref[lo:lo + m, b * tokens:(b + 1) * tokens]
            right_op = r_ref[ro:ro + nw, b * tokens:(b + 1) * tokens]
            g = mm(left_op, right_op, NT)
            if nw < COLS:
                g = jnp.concatenate([g, jnp.zeros((m, COLS - nw), F32)], axis=1) if nw % LANES == 0 else jnp.pad(g, ((0, 0), (0, COLS - nw)))
            blocks.append(g)
        return blocks

    for b in range(images):
        cp_x(b).wait()

        def qk_body(t, _):
            off = pl.multiple_of(b * tokens + t * TOK, TOK)
            xt = x_v[pl.ds(off, TOK), :].astype(F32)
            x_hat, _inv = norm(xt)
            u = (x_hat * gain_row + bias_row).astype(BF16)
            u_t = u.T
            ut[:, pl.ds(off, TOK)] = u_t
            for m in range(2):
                z = mm(wt_v[m * dim:(m + 1) * dim, :], ut[:, pl.ds(off, TOK)]).astype(BF16)
                zt[m * dim:(m + 1) * dim, pl.ds(off, TOK)] = z
                zf = z.astype(F32)
                sq = zf * zf
                tot = sq[:, 0:LANES]
                for j in range(1, TOK // LANES):
                    tot = tot + sq[:, j * LANES:(j + 1) * LANES]
                sq_acc[b, m] += tot
            return 0
        lax.fori_loop(0, tiles, qk_body, 0)
        to_pairs(gram(b, zt, 0, zt, dim), gs_out.at[b])
        q_row = jnp.sum(sq_acc[b, 0].T, axis=0, keepdims=True)
        k_row = jnp.sum(sq_acc[b, 1].T, axis=0, keepdims=True)
        sub8 = lax.broadcasted_iota(jnp.int32, (8, dim), 0)
        qk = jnp.where(sub8 == 0, q_row, jnp.where(sub8 == 1, k_row, 0.0))
        for d in range(n):
            s0 = d * per_dev
            base = s0 // LANES * LANES
            if base + COLS <= dim:
                wide = qk[:, base:base + COLS]
                if s0 - base:
                    wide = pltpu.roll(wide, COLS - (s0 - base), 1)
                piece = wide[:, :LANES]
            else:
                base = dim - COLS
                wide = pltpu.roll(qk[:, base:dim], COLS - (s0 - base), 1)
                piece = wide[:, :LANES]
            gs_out[b, d, hd:hd + 8, :] = piece
        if b == 0:
            pl.semaphore_wait(barrier, n - 1)
        for k in range(1, n):
            dst = (me + k) % n
            rcopy(gs_out.at[b, dst], gs_in.at[b, k - 1], gs_s.at[b, k - 1], gs_r.at[b, k - 1], dst).start()

    def v_body(t, _):
        off = pl.multiple_of(t * TOK, TOK)
        zt[2 * dim:3 * dim, pl.ds(off, TOK)] = mm(wt_v[2 * dim:3 * dim, :], ut[:, pl.ds(off, TOK)]).astype(BF16)
        return 0
    lax.fori_loop(0, images * tiles, v_body, 0)

    eye = lax.broadcasted_iota(jnp.int32, (hd, hd), 0) == lax.broadcasted_iota(jnp.int32, (hd, hd), 1)

    def col_of(row):
        return jnp.sum(jnp.where(eye, row, 0.0), axis=1, keepdims=True)

    def row_of(col):
        return jnp.sum(jnp.where(eye, col, 0.0), axis=0, keepdims=True)

    def attn_state(b, s):
        blk = gs_sum[b]
        sl = slice(s * hd, (s + 1) * hd)
        g = blk[0:hd, sl]
        qr = blk[hd:hd + 1, sl]
        kr = blk[hd + 1:hd + 2, sl]
        unit = lax.rsqrt(col_of(qr)) * lax.rsqrt(kr)
        tau = tau_ref[me * 2 + s]
        cosine = g * unit
        logits = tau * cosine
        e = jnp.exp(logits - jnp.max(logits, axis=-1, keepdims=True))
        probs = e / jnp.sum(e, axis=-1, keepdims=True)
        return cosine, logits, probs, tau * unit, qr, kr

    def pair(a0, a1):
        r = a0.shape[0]
        z = jnp.zeros((r, LANES - 2 * hd), a0.dtype)
        return jnp.concatenate([a0, a1, z], axis=1)

    def owner_forward(b):
        for k in range(1, n):
            rcopy(gs_out.at[b, 0], gs_in.at[b, k - 1], gs_s.at[b, k - 1], gs_r.at[b, k - 1], me).wait_recv()
        tot = gs_out[b, me]
        for k in range(1, n):
            tot = tot + gs_in[b, k - 1]
        gs_sum[b] = tot
        p0 = attn_state(b, 0)[2]
        p1 = attn_state(b, 1)[2]
        a_all[b, me] = pair(p0, p1).astype(BF16)
        for k in range(1, n):
            dst = (me + k) % n
            rcopy(a_all.at[b, me], a_all.at[b, me], a_s.at[b, k - 1], a_r.at[b, k - 1], dst).start()

    def owner_backward(b):
        for k in range(1, n):
            rcopy(ds_out.at[b, 0], ds_in.at[b, k - 1], ds_s.at[b, k - 1], ds_r.at[b, k - 1], me).wait_recv()
        tot = ds_out[b, me]
        for k in range(1, n):
            tot = tot + ds_in[b, k - 1]
        tot = tot.astype(BF16).astype(F32)
        gs, qs, ks, ts = [], [], [], []
        for s in range(2):
            cosine, logits, probs, scale, qr, kr = attn_state(b, s)
            dp = tot[:, s * hd:(s + 1) * hd]
            gl = probs * (dp - jnp.sum(probs * dp, axis=-1, keepdims=True))
            weighted = gl * logits
            gs.append(gl * scale)
            qs.append(-row_of(jnp.sum(weighted, axis=1, keepdims=True)) / qr)
            ks.append(-jnp.sum(weighted, axis=0, keepdims=True) / kr)
            ts.append(jnp.sum(jnp.sum(gl * cosine, axis=1, keepdims=True), axis=0, keepdims=True))
        g_all[b, me] = pair(gs[0], gs[1]).astype(BF16)
        sub = lax.broadcasted_iota(jnp.int32, (8, LANES), 0)
        lane = lax.broadcasted_iota(jnp.int32, (8, LANES), 1)
        taus = jnp.where(lane == 0, ts[0], jnp.where(lane == 1, ts[1], 0.0))
        c_all[b, me] = jnp.where(sub == 0, pair(qs[0], qs[1]), jnp.where(sub == 1, pair(ks[0], ks[1]), jnp.where(sub == 2, taus, 0.0)))
        for k in range(1, n):
            dst = (me + k) % n
            rcopy(g_all.at[b, me], g_all.at[b, me], g_s.at[b, k - 1], g_r.at[b, k - 1], dst).start()
            rcopy(c_all.at[b, me], c_all.at[b, me], c_s.at[b, k - 1], c_r.at[b, k - 1], dst).start()

    def gathered(ref, ss, rs, b):
        for k in range(1, n):
            src = (me + n - k) % n
            rcopy(ref.at[b, me], ref.at[b, src], ss.at[b, k - 1], rs.at[b, k - 1], me).wait_recv()

    def grad_heads(b):
        cp_dy(b).wait()
        if b == 0:
            cp_wo.wait()

        def body(t, _):
            off = pl.multiple_of(b * tokens + t * TOK, TOK)
            dot_v[:, pl.ds(off, TOK)] = mm(wo_v[...], dy_v[pl.ds(off, TOK), :], NT).astype(BF16)
            return 0
        lax.fori_loop(0, tiles, body, 0)
        to_pairs(gram(b, dot_v, 0, zt, 2 * dim), ds_out.at[b])
        for k in range(1, n):
            dst = (me + k) % n
            rcopy(ds_out.at[b, dst], ds_in.at[b, k - 1], ds_s.at[b, k - 1], ds_r.at[b, k - 1], dst).start()

    sj = lax.broadcasted_iota(jnp.int32, (LANES, COLS), 0)
    slane = lax.broadcasted_iota(jnp.int32, (LANES, COLS), 1)
    sels = []
    for s in range(2):
        hit = jnp.zeros((LANES, COLS), jnp.bool_)
        for k in range(wheads):
            hit = jnp.logical_or(hit, slane - k * hd == sj - s * hd)
        hit = jnp.logical_and(hit, jnp.logical_and(sj >= s * hd, sj < (s + 1) * hd))
        sels.append(jnp.where(hit, 1.0, 0.0).astype(BF16))
    blane = lax.broadcasted_iota(jnp.int32, (hd, COLS), 1)

    def build(ref, b):
        flat = ref[b].reshape(n * hd, LANES)
        for s in range(2):
            spread = mm(flat, sels[s])
            for d in range(n):
                w, k = divmod(2 * d + s, wheads)
                blk = jnp.where(jnp.logical_and(blane >= k * hd, blane < (k + 1) * hd), spread[d * hd:(d + 1) * hd], 0.0)
                bd[b, w, 0, k * hd:(k + 1) * hd, :] = blk.astype(BF16)
        for w in range(nwin):
            bd[b, w, 1] = bd[b, w, 0].T

    def windows():
        for w in range(nwin):
            r0 = w * wrow
            yield w, r0, min(wrow, dim - r0), min(COLS, dim - r0)

    def out_and_dv(b):
        def body(t, _):
            off = pl.multiple_of(b * tokens + t * TOK, TOK)
            for w, r0, m, kk in windows():
                ot[r0:r0 + m, pl.ds(off, TOK)] = mm(bd[b, w, 0, 0:m, 0:kk], zt[2 * dim + r0:2 * dim + r0 + kk, pl.ds(off, TOK)]).astype(BF16)
            for w, r0, m, kk in windows():
                zt[2 * dim + r0:2 * dim + r0 + m, pl.ds(off, TOK)] = mm(bd[b, w, 1, 0:m, 0:kk], dot_v[r0:r0 + kk, pl.ds(off, TOK)]).astype(BF16)
            return 0
        lax.fori_loop(0, tiles, body, 0)

    def dq_and_dk(b):
        ct = c_all[b].reshape(n * 8, LANES).T
        for d in range(n):
            colq[d * per_dev:(d + 1) * per_dev, :] = jnp.broadcast_to(ct[0:per_dev, 8 * d:8 * d + 1], (per_dev, LANES))
            colk[d * per_dev:(d + 1) * per_dev, :] = jnp.broadcast_to(ct[0:per_dev, 8 * d + 1:8 * d + 2], (per_dev, LANES))

        def body(t, _):
            off = pl.multiple_of(b * tokens + t * TOK, TOK)
            for w, r0, m, kk in windows():
                qw = zt[r0:r0 + kk, pl.ds(off, TOK)]
                kw = zt[dim + r0:dim + r0 + kk, pl.ds(off, TOK)]
                cq = jnp.concatenate([colq[r0:r0 + m, :]] * (TOK // LANES), axis=1)
                ck = jnp.concatenate([colk[r0:r0 + m, :]] * (TOK // LANES), axis=1)
                dq = mm(bd[b, w, 0, 0:m, 0:kk], kw) + cq * qw[0:m].astype(F32)
                dk = mm(bd[b, w, 1, 0:m, 0:kk], qw) + ck * kw[0:m].astype(F32)
                zt[r0:r0 + m, pl.ds(off, TOK)] = dq.astype(BF16)
                zt[dim + r0:dim + r0 + m, pl.ds(off, TOK)] = dk.astype(BF16)
            return 0
        lax.fori_loop(0, tiles, body, 0)

    def put_part(c, val):
        for j in range(n):
            part[c, j % 2, j // 2] = val[j * per_dev:(j + 1) * per_dev, :]

    def d2d(c):
        return rcopy(part.at[c, 1 - core], r1.at[c], d2d_s.at[c], d2d_r.at[c], partner)

    half = per_dev // 2

    def hop1(c):
        return (rcopy(r1.at[c, co, pl.ds(0, half)], r2.at[c, 0], p1_s.at[c, 0], p1_r.at[c, 0], right),
                rcopy(r1.at[c, co, pl.ds(half, half)], r2.at[c, 1], p1_s.at[c, 1], p1_r.at[c, 1], left))

    def hop2(c):
        return (rcopy(r1.at[c, cr], r3.at[c, 0], p2_s.at[c, 0], p2_r.at[c, 0], right),
                rcopy(r1.at[c, cl], r3.at[c, 1], p2_s.at[c, 1], p2_r.at[c, 1], left))

    def serve1(c):
        d2d(c).wait_recv()
        for blk in (co, cr, cl, chip):
            r1[c, blk] += part[c, core, blk]
        for h in hop1(c):
            h.start()

    def serve2(c):
        for h in hop1(c):
            h.wait_recv()
        r1[c, cr, 0:half] += r2[c, 0]
        r1[c, cl, half:per_dev] += r2[c, 1]
        for h in hop2(c):
            h.start()

    def serve3(c):
        for h in hop2(c):
            h.wait_recv()
        return (r1[c, chip] + r3[c, 0] + r3[c, 1]).astype(BF16)

    def wo_chunk(c, _):
        off = pl.multiple_of(c * COLS, COLS)
        put_part(c, mm(ot[...], dy_v[:, pl.ds(off, COLS)]))
        d2d(c).start()
        return 0

    def qkv_chunk(c, base):
        off = pl.multiple_of(base + c * COLS, COLS)
        put_part(c, mm(ut[...], zt[pl.ds(off, COLS), :], NT))
        d2d(c).start()

    owner_forward(0)
    grad_heads(0)
    owner_forward(1)
    grad_heads(1)
    gathered(a_all, a_s, a_r, 0)
    build(a_all, 0)
    out_and_dv(0)
    gathered(a_all, a_s, a_r, 1)
    build(a_all, 1)
    out_and_dv(1)
    owner_backward(0)
    wo_chunk(0, 0)

    def wo_loop(c, _):
        wo_chunk(c, 0)
        serve1(c - 1)
        return 0
    lax.fori_loop(1, o_chunks, wo_loop, 0)
    owner_backward(1)

    def v_loop(c, _):
        qkv_chunk(c, 2 * dim - o_chunks * COLS)
        serve1(c - 1)
        return 0
    lax.fori_loop(o_chunks, 2 * o_chunks, v_loop, 0)

    def s2_body(c, _):
        serve2(c)
        return 0
    lax.fori_loop(0, o_chunks, s2_body, 0)
    for b in range(images):
        gathered(g_all, g_s, g_r, b)
        gathered(c_all, c_s, c_r, b)
        build(g_all, b)
        dq_and_dk(b)

    def qk_loop(c, _):
        qkv_chunk(c, -2 * o_chunks * COLS)
        serve1(c - 1)
        return 0
    lax.fori_loop(2 * o_chunks, chunks, qk_loop, 0)
    serve1(chunks - 1)
    lax.fori_loop(o_chunks, chunks - 3, s2_body, 0)

    def y_copy(t):
        b = t // tiles
        return pltpu.make_async_copy(y_st.at[t], y_hbm.at[b, pl.ds(pl.multiple_of((t % tiles) * TOK, TOK), TOK)], out_sem.at[0, t])

    def dx_copy(t):
        b = t // tiles
        return pltpu.make_async_copy(x_v.at[pl.ds(pl.multiple_of(t * TOK, TOK), TOK)], dx_hbm.at[b, pl.ds(pl.multiple_of((t % tiles) * TOK, TOK), TOK)], out_sem.at[1, t])

    def y_body(t, _):
        off = pl.multiple_of(t * TOK, TOK)
        o = ot[:, pl.ds(off, TOK)].T
        y_st[t] = (x_v[pl.ds(off, TOK), :].astype(F32) + mm(o, wo_v[...])).astype(BF16)
        y_copy(t).start()
        return 0
    lax.fori_loop(0, images * tiles, y_body, 0)
    lax.fori_loop(chunks - 3, chunks, s2_body, 0)

    def dx_body(t, _):
        off = pl.multiple_of(t * TOK, TOK)
        du = mm(w_v[...], zt[:, pl.ds(off, TOK)]).astype(BF16).T.astype(F32)
        x_hat, inv = norm(x_v[pl.ds(off, TOK), :].astype(F32))
        prod = du * x_hat
        dgb[0] += jnp.sum(prod.reshape(TOK // 8, 8, dim), axis=0)
        dgb[1] += jnp.sum(du.reshape(TOK // 8, 8, dim), axis=0)
        a9 = du * gain_row
        m1 = jnp.sum(a9, axis=-1, keepdims=True) * (1.0 / dim)
        m2 = jnp.sum(a9 * x_hat, axis=-1, keepdims=True) * (1.0 / dim)
        gx = inv * (a9 - m1 - x_hat * m2)
        x_v[pl.ds(off, TOK), :] = (dy_v[pl.ds(off, TOK), :].astype(F32) + gx).astype(BF16)
        dx_copy(t).start()
        return 0
    lax.fori_loop(0, images * tiles, dx_body, 0)

    sub8 = lax.broadcasted_iota(jnp.int32, (8, dim), 0)
    gb = jnp.where(sub8 == 0, jnp.sum(dgb[0], axis=0, keepdims=True), jnp.where(sub8 == 1, jnp.sum(dgb[1], axis=0, keepdims=True), 0.0))
    gb_all[me] = gb
    for k in range(1, n):
        dst = (me + k) % n
        rcopy(gb_all.at[me], gb_all.at[me], gb_s.at[k - 1], gb_r.at[k - 1], dst).start()

    lane = lax.broadcasted_iota(jnp.int32, (1, LANES), 1)
    dtau = jnp.zeros((1, LANES), F32)
    for d in range(n):
        row = c_all[0, d, 2:3, :]
        for b in range(1, images):
            row = row + c_all[b, d, 2:3, :]
        if d:
            row = pltpu.roll(row, 2 * d, 1)
        dtau = jnp.where(jnp.logical_and(lane >= 2 * d, lane < 2 * d + 2), row, dtau)
    dtau_ref[...] = dtau

    def s3_wo(c, _):
        dwo_ref[:, pl.ds(pl.multiple_of(c * COLS, COLS), COLS)] = serve3(c)
        return 0
    lax.fori_loop(0, o_chunks, s3_wo, 0)

    def s3_v(c, _):
        dwqkv_ref[:, pl.ds(pl.multiple_of(2 * dim - dim + c * COLS, COLS), COLS)] = serve3(c)
        return 0
    lax.fori_loop(o_chunks, 2 * o_chunks, s3_v, 0)

    for k in range(1, n):
        src = (me + n - k) % n
        rcopy(gb_all.at[me], gb_all.at[src], gb_s.at[k - 1], gb_r.at[k - 1], me).wait_recv()
    tot = gb_all[0]
    for d in range(1, n):
        tot = tot + gb_all[d]
    dgain_ref[...] = tot[0:1, :]
    dbias_ref[...] = tot[1:2, :]

    def s3_qk(c, _):
        dwqkv_ref[:, pl.ds(pl.multiple_of(c * COLS - 2 * dim, COLS), COLS)] = serve3(c)
        return 0
    lax.fori_loop(2 * o_chunks, chunks, s3_qk, 0)

    for b in range(images):
        for k in range(1, n):
            rcopy(gs_out.at[b, 0], gs_in.at[b, k - 1], gs_s.at[b, k - 1], gs_r.at[b, k - 1], me).wait_send()
            rcopy(a_all.at[b, me], a_all.at[b, me], a_s.at[b, k - 1], a_r.at[b, k - 1], me).wait_send()
            rcopy(ds_out.at[b, 0], ds_in.at[b, k - 1], ds_s.at[b, k - 1], ds_r.at[b, k - 1], me).wait_send()
            rcopy(g_all.at[b, me], g_all.at[b, me], g_s.at[b, k - 1], g_r.at[b, k - 1], me).wait_send()
            rcopy(c_all.at[b, me], c_all.at[b, me], c_s.at[b, k - 1], c_r.at[b, k - 1], me).wait_send()
    for k in range(1, n):
        rcopy(gb_all.at[me], gb_all.at[me], gb_s.at[k - 1], gb_r.at[k - 1], me).wait_send()

    def drain(c, _):
        d2d(c).wait_send()
        for h in hop1(c) + hop2(c):
            h.wait_send()
        return 0
    lax.fori_loop(0, chunks, drain, 0)

    def drain_out(t, _):
        y_copy(t).wait()
        dx_copy(t).wait()
        return 0
    lax.fori_loop(0, images * tiles, drain_out, 0)


def solution(mesh):
    n = mesh.shape["sp"]

    def local_step(x_in, grad_y, ln_gain, ln_bias, w_qkv, w_out, temp_tau):
        images, tokens, dim = x_in.shape
        heads = temp_tau.shape[0]
        hd = dim // heads
        rows = images * tokens
        per_dev = dim // n
        chunks = 4 * dim // COLS
        nwin = -(-heads // (COLS // hd))
        any_spec = pl.BlockSpec(memory_space=pl.ANY)
        vmem = pl.BlockSpec(memory_space=pltpu.VMEM)
        smem = pl.BlockSpec(memory_space=pltpu.SMEM)
        dma = pltpu.SemaphoreType.DMA
        pairs = (images, n - 1)
        out = pl.pallas_call(
            functools.partial(xca_kernel, n, heads),
            out_shape=(
                jax.ShapeDtypeStruct(x_in.shape, BF16),
                jax.ShapeDtypeStruct(x_in.shape, BF16),
                jax.ShapeDtypeStruct((per_dev, 3 * dim), BF16),
                jax.ShapeDtypeStruct((per_dev, dim), BF16),
                jax.ShapeDtypeStruct((1, dim), F32),
                jax.ShapeDtypeStruct((1, dim), F32),
                jax.ShapeDtypeStruct((1, LANES), F32),
            ),
            in_specs=[any_spec, any_spec, vmem, vmem, any_spec, any_spec, smem],
            out_specs=(any_spec, any_spec, vmem, vmem, vmem, vmem, vmem),
            scratch_shapes=[
                pltpu.VMEM((rows, dim), BF16),
                pltpu.VMEM((rows, dim), BF16),
                pltpu.VMEM((dim, 3 * dim), BF16),
                pltpu.VMEM((3 * dim, dim), BF16),
                pltpu.VMEM((dim, dim), BF16),
                pltpu.VMEM((dim, rows), BF16),
                pltpu.VMEM((3 * dim, rows), BF16),
                pltpu.VMEM((dim, rows), BF16),
                pltpu.VMEM((dim, rows), BF16),
                pltpu.VMEM((rows // TOK, TOK, dim), BF16),
                pltpu.VMEM((images, 2, dim, LANES), F32),
                pltpu.VMEM((images, n, hd + 8, LANES), F32),
                pltpu.VMEM((images, n - 1, hd + 8, LANES), F32),
                pltpu.VMEM((images, hd + 8, LANES), F32),
                pltpu.VMEM((images, n, hd, LANES), BF16),
                pltpu.VMEM((images, n, hd, LANES), F32),
                pltpu.VMEM((images, n - 1, hd, LANES), F32),
                pltpu.VMEM((images, n, hd, LANES), BF16),
                pltpu.VMEM((images, n, 8, LANES), F32),
                pltpu.VMEM((images, nwin, 2, COLS, COLS), BF16),
                pltpu.VMEM((dim, LANES), F32),
                pltpu.VMEM((dim, LANES), F32),
                pltpu.VMEM((2, 8, dim), F32),
                pltpu.VMEM((8, dim), F32),
                pltpu.VMEM((n, 8, dim), F32),
                pltpu.VMEM((chunks, 2, n // 2, per_dev, COLS), F32),
                pltpu.VMEM((chunks, n // 2, per_dev, COLS), F32),
                pltpu.VMEM((chunks, 2, per_dev // 2, COLS), F32),
                pltpu.VMEM((chunks, 2, per_dev, COLS), F32),
                dma((6,)), dma((2, rows // TOK)),
                dma((chunks,)), dma((chunks,)),
                dma((chunks, 2)), dma((chunks, 2)), dma((chunks, 2)), dma((chunks, 2)),
                dma(pairs), dma(pairs), dma(pairs), dma(pairs), dma(pairs), dma(pairs),
                dma(pairs), dma(pairs), dma(pairs), dma(pairs),
                dma((n - 1,)), dma((n - 1,)),
            ],
            compiler_params=pltpu.CompilerParams(
                collective_id=0, has_side_effects=True, vmem_limit_bytes=67043328),
            name="xca_block",
        )(x_in, grad_y, ln_gain.reshape(1, dim), ln_bias.reshape(1, dim), w_qkv, w_out, temp_tau)
        y, dx, dwqkv, dwo, dgain, dbias, dtau = out
        return y, dx, dwqkv, dwo, dgain.reshape(dim), dbias.reshape(dim), dtau[0, :heads]

    tok = P("dp", "sp", None)
    return jax.shard_map(
        local_step, mesh=mesh,
        in_specs=(tok, tok, P(), P(), P(), P(), P()),
        out_specs=(tok, tok, P(("dp", "sp"), None), P(("dp", "sp"), None), P("dp"), P("dp"), P("dp")),
        check_vma=False)
```

profile of v0, /device:TPU:113, one launch (start us, length us, event | category | flops | bytes accessed | tf_op | source)
XLA Modules:
  0.0 95.4 jit_solution(14151405883127248370)
XLA Ops:
  0.6 1.3 %reshape.26.gain_ref = f32[1,768]{1,0:T(1,128)} reshape(f32[768]{0:T(1024)} %param.9) | data formatting | bytes 6144 | tf_op jit(solution)/shard_map/reshape | solution.py:582
  1.9 1.3 %reshape.27.bias_ref = f32[1,768]{1,0:T(1,128)} reshape(f32[768]{0:T(1024)} %param.10) | data formatting | bytes 6144 | tf_op jit(solution)/shard_map/reshape | solution.py:582
  3.2 81.5 %xca_block.1 = (bf16[2,1024,768]{2,1,0:T(8,128)(2,1)}, bf16[2,1024,768]{2,1,0:T(8,128)(2,1)}, bf16[96,2304]{1,0:T(8,128)(2,1)}, bf16[96,768]{1,0:T(8,128)(2,1)},...) custom-call(bf16[2,1024,768]{2,1,0:T(8,128)(2,1)} %x_hbm.1, bf16[2,1024,768]{2,1,0:T(8,128)(2,1)} %dy_hbm.1, ...), custom_call_target="tpu_custom_call" | custom-call | tf_op jit(solution)/shard_map/xca_block/pallas_call | solution.py:529
  84.7 1.3 %reduce = f32[768]{0:T(1024)} reduce(f32[1,768]{1,0:T(1,128)} %get-tuple-element.18, f32[]{:T(128)} %constant), dimensions={0}, to_apply=%get-tuple-element.18.reduce_sub_computation | reduce | bytes 6148 | tf_op jit(solution)/shard_map/xca_block/pallas_call | solution.py:529
  86.0 1.3 %reduce.1 = f32[768]{0:T(1024)} reduce(f32[1,768]{1,0:T(1,128)} %get-tuple-element.19, f32[]{:T(128)} %constant), dimensions={0}, to_apply=%get-tuple-element.19.reduce_sub_computation | reduce | bytes 6148 | tf_op jit(solution)/shard_map/xca_block/pallas_call | solution.py:529
  87.2 1.2 %slice_bitcast_fusion = f32[16]{0:T(128)} fusion(f32[1,128]{1,0:T(1,128)} %get-tuple-element.20), kind=kLoop, calls=%fused_computation | loop fusion | bytes 128 | tf_op jit(solution)/shard_map/squeeze | solution.py:584
  88.4 0.0 copy-start
  88.4 3.9 %copy.18 = bf16[2,1024,768]{2,1,0:T(8,128)(2,1)} copy(bf16[2,1024,768]{2,1,0:T(8,128)(2,1)} %get-tuple-element.28) | data formatting | bytes 6291456
  92.3 0.0 copy-done
  92.3 0.0 copy-start.1
  92.3 0.0 copy-start.2
  92.3 1.7 %copy.19 = bf16[2,1024,768]{2,1,0:T(8,128)(2,1)} copy(bf16[2,1024,768]{2,1,0:T(8,128)(2,1)S(1)} %copy-done) | data formatting | bytes 6291456
  94.0 0.0 copy-done.1
  94.0 0.8 copy.20
  94.8 0.0 copy-done.2
  94.8 0.7 copy.21
Async XLA Ops:
  88.4 3.9 %copy-start = (bf16[2,1024,768]{2,1,0:T(8,128)(2,1)S(1)}, bf16[2,1024,768]{2,1,0:T(8,128)(2,1)}, u32[]{:S(2)}) copy-start(bf16[2,1024,768]{2,1,0:T(8,128)(2,1)} %get-tuple-element.29) | copy-start | bytes 9437188
  92.3 1.7 %copy-start.1 = (bf16[96,2304]{1,0:T(8,128)(2,1)S(1)}, bf16[96,2304]{1,0:T(8,128)(2,1)}, u32[]{:S(2)}) copy-start(bf16[96,2304]{1,0:T(8,128)(2,1)} %get-tuple-element.30) | copy-start | bytes 1327108
  92.3 2.4 %copy-start.2 = (bf16[96,768]{1,0:T(8,128)(2,1)S(1)}, bf16[96,768]{1,0:T(8,128)(2,1)}, u32[]{:S(2)}) copy-start(bf16[96,768]{1,0:T(8,128)(2,1)} %get-tuple-element.31) | copy-start | bytes 442372
where the time goes:
time: 95.7 us; the launch traced here: 95.4 us
  Pallas kernels  81.5 us (85%)
  local copies, waits for them, and re-layouts  10.7 us (11%)
  other arithmetic  2.56 us (3%)
    pallas_call x1, Pallas kernels, local_step(): pl.pallas_call(functools.partial(xca_kernel, n, heads), out_shape=(jax.Sh...  81.5 us
    unnamed x10, local copies, waits for them, and re-layouts  7 us
    pallas_call x2, other arithmetic, local_step(): pl.pallas_call(functools.partial(xca_kernel, n, heads), out_shape=(jax.Sh...  2.56 us

commit v1 on v0

--- a/solution.py
+++ b/solution.py
@@ -23,10 +23,10 @@
 
 def xca_kernel(
     n, heads,
-    x_hbm, dy_hbm, gain_ref, bias_ref, wqkv_hbm, wo_hbm, tau_ref,
+    x_hbm, dy_hbm, gain_hbm, bias_hbm, wqkv_hbm, wo_hbm, tau_hbm,
     y_hbm, dx_hbm, dwqkv_ref, dwo_ref, dgain_ref, dbias_ref, dtau_ref,
-    x_v, dy_v, w_v, wt_v, wo_v, ut, zt, dot_v, ot, y_st,
-    sq_acc, gs_out, gs_in, gs_sum, a_all, ds_out, ds_in, g_all, c_all, bd, colq, colk, dgb, gb_out, gb_all,
+    gain_ref, bias_ref, tau_ref, x_v, dy_v, w_v, wt_v, wo_v, ut, zt, dot_v, ot,
+    sq_acc, gs_out, gs_in, gs_sum, a_all, ds_out, ds_in, g_all, c_all, bd, colq, colk, dgb, gb_all,
     part, r1, r2, r3,
     in_sem, out_sem, d2d_s, d2d_r, p1_s, p1_r, p2_s, p2_r,
     gs_s, gs_r, a_s, a_r, ds_s, ds_r, g_s, g_r, c_s, c_r, gb_s, gb_r,
@@ -49,42 +49,42 @@
     partner = chip * 2 + (1 - core)
     cr, cl, co = (chip + 1) % chips, (chip + chips - 1) % chips, (chip + 2) % chips
 
+    far_first = sorted(range(1, n), key=lambda k: abs(2 * k - n))
+
     def rcopy(src, dst, ss, rs, dev):
         return pltpu.make_async_remote_copy(
             src_ref=src, dst_ref=dst, send_sem=ss, recv_sem=rs,
             device_id={"sp": dev}, device_id_type=pl.DeviceIdType.MESH)
 
-    def cp_x(b):
-        return pltpu.make_async_copy(x_hbm.at[b], x_v.at[pl.ds(b * tokens, tokens)], in_sem.at[b])
+    def cp_x(b, t):
+        return pltpu.make_async_copy(x_hbm.at[b, pl.ds(t * TOK, TOK)], x_v.at[pl.ds(b * tokens + t * TOK, TOK)], in_sem.at[b * tiles + t])
 
     def cp_dy(b):
-        return pltpu.make_async_copy(dy_hbm.at[b], dy_v.at[pl.ds(b * tokens, tokens)], in_sem.at[2 + b])
-
-    cp_w = pltpu.make_async_copy(wqkv_hbm, w_v, in_sem.at[4])
-    cp_wo = pltpu.make_async_copy(wo_hbm, wo_v, in_sem.at[5])
-    cp_w.start()
-    cp_x(0).start()
-    cp_x(1).start()
-    cp_wo.start()
-    cp_dy(0).start()
-    cp_dy(1).start()
+        return pltpu.make_async_copy(dy_hbm.at[b], dy_v.at[pl.ds(b * tokens, tokens)], in_sem.at[images * tiles + b])
+
+    base = images * tiles + images
+    cp_small = [pltpu.make_async_copy(h, v, in_sem.at[base + i]) for i, (h, v) in enumerate(
+        ((gain_hbm, gain_ref), (bias_hbm, bias_ref), (tau_hbm, tau_ref)))]
+    base += 3
+    cp_wqk = pltpu.make_async_copy(wqkv_hbm.at[:, pl.ds(0, 2 * dim)], w_v.at[:, pl.ds(0, 2 * dim)], in_sem.at[base])
+    cp_wv = pltpu.make_async_copy(wqkv_hbm.at[:, pl.ds(2 * dim, dim)], w_v.at[:, pl.ds(2 * dim, dim)], in_sem.at[base + 1])
+    cp_wo = pltpu.make_async_copy(wo_hbm, wo_v, in_sem.at[base + 2])
+    for c in cp_small:
+        c.start()
+    cp_x(0, 0).start()
+    cp_wqk.start()
+    cp_x(0, 1).start()
 
     barrier = pltpu.get_barrier_semaphore()
     for k in range(1, n):
         pl.semaphore_signal(barrier, inc=1, device_id={"sp": (me + k) % n},
                             device_id_type=pl.DeviceIdType.MESH)
-
     sq_acc[...] = jnp.zeros_like(sq_acc)
     bd[...] = jnp.zeros_like(bd)
     dgb[...] = jnp.zeros_like(dgb)
-
-    cp_w.wait()
-
-    def wt_body(i, _):
-        off = pl.multiple_of(i * COLS, COLS)
-        wt_v[pl.ds(off, COLS), :] = w_v[:, pl.ds(off, COLS)].T
-        return 0
-    lax.fori_loop(0, 3 * dim // COLS, wt_body, 0)
+    for c in cp_small:
+        c.wait()
+    cp_x(0, 0).wait()
 
     def norm(xt):
         mean = jnp.sum(xt, axis=-1, keepdims=True) * (1.0 / dim)
@@ -92,12 +92,23 @@
         inv = lax.rsqrt(jnp.sum(cen * cen, axis=-1, keepdims=True) * (1.0 / dim) + LN_EPS)
         return cen * inv, inv
 
-    gain_row = gain_ref[...]
-    bias_row = bias_ref[...]
+    gain_row = gain_ref[...].reshape(1, dim)
+    bias_row = bias_ref[...].reshape(1, dim)
+
+    def norm_rows(r0, count):
+        x_hat, _inv = norm(x_v[pl.ds(r0, count), :].astype(F32))
+        ut[:, pl.ds(r0, count)] = (x_hat * gain_row + bias_row).astype(BF16).T
+
+    def transpose_w(c0, count):
+        def body(i, _):
+            off = pl.multiple_of(c0 + i * COLS, COLS)
+            wt_v[pl.ds(off, COLS), :] = w_v[:, pl.ds(off, COLS)].T
+            return 0
+        lax.fori_loop(0, count // COLS, body, 0)
 
     lane_w = lax.broadcasted_iota(jnp.int32, (hd, LANES), 1)
 
-    def to_pairs(blocks, out_ref):
+    def to_pairs(blocks, out_ref, extra=None):
         for d in range(n):
             picked = []
             for s in range(2):
@@ -107,7 +118,13 @@
                 if shift:
                     strip = pltpu.roll(strip, shift, 1)
                 picked.append(strip[:, :LANES])
-            out_ref[d, 0:hd, :] = jnp.where(lane_w < hd, picked[0], jnp.where(lane_w < 2 * hd, picked[1], 0.0))
+            rest = 0.0
+            if extra is not None:
+                for i, col in enumerate(extra):
+                    for s in range(2):
+                        r0 = (2 * d + s) * hd
+                        rest = jnp.where(lane_w == 2 * hd + 2 * i + s, col[r0:r0 + hd], rest)
+            out_ref[d] = jnp.where(lane_w < hd, picked[0], jnp.where(lane_w < 2 * hd, picked[1], rest))
 
     def gram(b, l_ref, l0, r_ref, r0):
         blocks = []
@@ -119,82 +136,88 @@
             right_op = r_ref[ro:ro + nw, b * tokens:(b + 1) * tokens]
             g = mm(left_op, right_op, NT)
             if nw < COLS:
-                g = jnp.concatenate([g, jnp.zeros((m, COLS - nw), F32)], axis=1) if nw % LANES == 0 else jnp.pad(g, ((0, 0), (0, COLS - nw)))
+                g = jnp.pad(g, ((0, 0), (0, COLS - nw)))
             blocks.append(g)
         return blocks
 
-    for b in range(images):
-        cp_x(b).wait()
-
-        def qk_body(t, _):
-            off = pl.multiple_of(b * tokens + t * TOK, TOK)
-            xt = x_v[pl.ds(off, TOK), :].astype(F32)
-            x_hat, _inv = norm(xt)
-            u = (x_hat * gain_row + bias_row).astype(BF16)
-            u_t = u.T
-            ut[:, pl.ds(off, TOK)] = u_t
-            for m in range(2):
-                z = mm(wt_v[m * dim:(m + 1) * dim, :], ut[:, pl.ds(off, TOK)]).astype(BF16)
-                zt[m * dim:(m + 1) * dim, pl.ds(off, TOK)] = z
-                zf = z.astype(F32)
-                sq = zf * zf
-                tot = sq[:, 0:LANES]
-                for j in range(1, TOK // LANES):
-                    tot = tot + sq[:, j * LANES:(j + 1) * LANES]
-                sq_acc[b, m] += tot
-            return 0
-        lax.fori_loop(0, tiles, qk_body, 0)
-        to_pairs(gram(b, zt, 0, zt, dim), gs_out.at[b])
-        q_row = jnp.sum(sq_acc[b, 0].T, axis=0, keepdims=True)
-        k_row = jnp.sum(sq_acc[b, 1].T, axis=0, keepdims=True)
-        sub8 = lax.broadcasted_iota(jnp.int32, (8, dim), 0)
-        qk = jnp.where(sub8 == 0, q_row, jnp.where(sub8 == 1, k_row, 0.0))
-        for d in range(n):
-            s0 = d * per_dev
-            base = s0 // LANES * LANES
-            if base + COLS <= dim:
-                wide = qk[:, base:base + COLS]
-                if s0 - base:
-                    wide = pltpu.roll(wide, COLS - (s0 - base), 1)
-                piece = wide[:, :LANES]
-            else:
-                base = dim - COLS
-                wide = pltpu.roll(qk[:, base:dim], COLS - (s0 - base), 1)
-                piece = wide[:, :LANES]
-            gs_out[b, d, hd:hd + 8, :] = piece
+    def qk_tile(off, following, wt_cols=None):
+        for m in range(2):
+            z = mm(wt_v[m * dim:(m + 1) * dim, :], ut[:, pl.ds(off, TOK)]).astype(BF16)
+            zt[m * dim:(m + 1) * dim, pl.ds(off, TOK)] = z
+            zf = z.astype(F32)
+            sq = zf * zf
+            tot = sq[:, 0:LANES]
+            for j in range(1, TOK // LANES):
+                tot = tot + sq[:, j * LANES:(j + 1) * LANES]
+            sq_acc[off // tokens, m * dim:(m + 1) * dim] += tot
+        if following is not None:
+            norm_rows(following, TOK)
+        if wt_cols is not None:
+            wt_v[wt_cols:wt_cols + dim // 2, :] = w_v[:, wt_cols:wt_cols + dim // 2].T
+
+    def send_gram(b):
+        cols = [jnp.sum(sq_acc[b, m * dim:(m + 1) * dim], axis=1, keepdims=True) for m in range(2)]
+        to_pairs(gram(b, zt, 0, zt, dim), gs_out.at[b], cols)
         if b == 0:
             pl.semaphore_wait(barrier, n - 1)
-        for k in range(1, n):
+        for k in far_first:
             dst = (me + k) % n
             rcopy(gs_out.at[b, dst], gs_in.at[b, k - 1], gs_s.at[b, k - 1], gs_r.at[b, k - 1], dst).start()
 
-    def v_body(t, _):
+    norm_rows(0, TOK)
+    cp_x(0, 1).wait()
+    cp_wqk.wait()
+    for b in range(1, images):
+        for t in range(tiles):
+            cp_x(b, t).start()
+    cp_wv.start()
+    cp_wo.start()
+    for b in range(images):
+        cp_dy(b).start()
+    transpose_w(0, 2 * dim)
+
+    def qk_first(t, _):
         off = pl.multiple_of(t * TOK, TOK)
-        zt[2 * dim:3 * dim, pl.ds(off, TOK)] = mm(wt_v[2 * dim:3 * dim, :], ut[:, pl.ds(off, TOK)]).astype(BF16)
-        return 0
-    lax.fori_loop(0, images * tiles, v_body, 0)
+        qk_tile(off, off + TOK)
+        return 0
+    for b in range(1, images):
+        for t in range(tiles):
+            cp_x(b, t).wait()
+    lax.fori_loop(0, tiles, qk_first, 0)
+    send_gram(0)
+    cp_wv.wait()
+    for t in range(tiles):
+        off = tokens + t * TOK
+        qk_tile(off, off + TOK if t + 1 < tiles else None, 2 * dim + t * dim // tiles)
+    send_gram(1)
+
+    def values(b):
+        def v_body(t, _):
+            off = pl.multiple_of(b * tokens + t * TOK, TOK)
+            zt[2 * dim:3 * dim, pl.ds(off, TOK)] = mm(wt_v[2 * dim:3 * dim, :], ut[:, pl.ds(off, TOK)]).astype(BF16)
+            return 0
+        lax.fori_loop(0, tiles, v_body, 0)
 
     eye = lax.broadcasted_iota(jnp.int32, (hd, hd), 0) == lax.broadcasted_iota(jnp.int32, (hd, hd), 1)
-
-    def col_of(row):
-        return jnp.sum(jnp.where(eye, row, 0.0), axis=1, keepdims=True)
 
     def row_of(col):
         return jnp.sum(jnp.where(eye, col, 0.0), axis=0, keepdims=True)
 
+    head_lane = lax.broadcasted_iota(jnp.int32, (1, heads), 1)
+    tau_row = tau_ref[...].reshape(1, heads)
+
     def attn_state(b, s):
         blk = gs_sum[b]
-        sl = slice(s * hd, (s + 1) * hd)
-        g = blk[0:hd, sl]
-        qr = blk[hd:hd + 1, sl]
-        kr = blk[hd + 1:hd + 2, sl]
-        unit = lax.rsqrt(col_of(qr)) * lax.rsqrt(kr)
-        tau = tau_ref[me * 2 + s]
+        g = blk[:, s * hd:(s + 1) * hd]
+        qc = blk[:, 2 * hd + s:2 * hd + s + 1]
+        kr = row_of(blk[:, 2 * hd + 2 + s:2 * hd + 3 + s])
+        unit = lax.rsqrt(qc) * lax.rsqrt(kr)
+        tau = jnp.sum(jnp.where(head_lane == me * 2 + s, tau_row, 0.0), axis=1, keepdims=True)
         cosine = g * unit
         logits = tau * cosine
         e = jnp.exp(logits - jnp.max(logits, axis=-1, keepdims=True))
         probs = e / jnp.sum(e, axis=-1, keepdims=True)
-        return cosine, logits, probs, tau * unit, qr, kr
+        return cosine, logits, probs, tau * unit, qc, kr
 
     def pair(a0, a1):
         r = a0.shape[0]
@@ -211,36 +234,39 @@
         p0 = attn_state(b, 0)[2]
         p1 = attn_state(b, 1)[2]
         a_all[b, me] = pair(p0, p1).astype(BF16)
-        for k in range(1, n):
+        for k in far_first:
             dst = (me + k) % n
             rcopy(a_all.at[b, me], a_all.at[b, me], a_s.at[b, k - 1], a_r.at[b, k - 1], dst).start()
 
-    def owner_backward(b):
-        for k in range(1, n):
-            rcopy(ds_out.at[b, 0], ds_in.at[b, k - 1], ds_s.at[b, k - 1], ds_r.at[b, k - 1], me).wait_recv()
-        tot = ds_out[b, me]
-        for k in range(1, n):
-            tot = tot + ds_in[b, k - 1]
-        tot = tot.astype(BF16).astype(F32)
-        gs, qs, ks, ts = [], [], [], []
-        for s in range(2):
-            cosine, logits, probs, scale, qr, kr = attn_state(b, s)
-            dp = tot[:, s * hd:(s + 1) * hd]
-            gl = probs * (dp - jnp.sum(probs * dp, axis=-1, keepdims=True))
-            weighted = gl * logits
-            gs.append(gl * scale)
-            qs.append(-row_of(jnp.sum(weighted, axis=1, keepdims=True)) / qr)
-            ks.append(-jnp.sum(weighted, axis=0, keepdims=True) / kr)
-            ts.append(jnp.sum(jnp.sum(gl * cosine, axis=1, keepdims=True), axis=0, keepdims=True))
-        g_all[b, me] = pair(gs[0], gs[1]).astype(BF16)
+    def owner_backward():
+        for b in range(images):
+            for k in range(1, n):
+                rcopy(ds_out.at[b, 0], ds_in.at[b, k - 1], ds_s.at[b, k - 1], ds_r.at[b, k - 1], me).wait_recv()
         sub = lax.broadcasted_iota(jnp.int32, (8, LANES), 0)
         lane = lax.broadcasted_iota(jnp.int32, (8, LANES), 1)
-        taus = jnp.where(lane == 0, ts[0], jnp.where(lane == 1, ts[1], 0.0))
-        c_all[b, me] = jnp.where(sub == 0, pair(qs[0], qs[1]), jnp.where(sub == 1, pair(ks[0], ks[1]), jnp.where(sub == 2, taus, 0.0)))
-        for k in range(1, n):
-            dst = (me + k) % n
-            rcopy(g_all.at[b, me], g_all.at[b, me], g_s.at[b, k - 1], g_r.at[b, k - 1], dst).start()
-            rcopy(c_all.at[b, me], c_all.at[b, me], c_s.at[b, k - 1], c_r.at[b, k - 1], dst).start()
+        for b in range(images):
+            tot = ds_out[b, me]
+            for k in range(1, n):
+                tot = tot + ds_in[b, k - 1]
+            tot = tot.astype(BF16).astype(F32)
+            gs, qs, ks, ts = [], [], [], []
+            for s in range(2):
+                cosine, logits, probs, scale, qc, kr = attn_state(b, s)
+                dp = tot[:, s * hd:(s + 1) * hd]
+                gl = probs * (dp - jnp.sum(probs * dp, axis=-1, keepdims=True))
+                weighted = gl * logits
+                gs.append(gl * scale)
+                qs.append(row_of(-jnp.sum(weighted, axis=1, keepdims=True) / qc))
+                ks.append(-jnp.sum(weighted, axis=0, keepdims=True) / kr)
+                ts.append(jnp.sum(jnp.sum(gl * cosine, axis=1, keepdims=True), axis=0, keepdims=True))
+            g_all[b, me] = pair(gs[0], gs[1]).astype(BF16)
+            taus = jnp.where(lane == 0, ts[0], jnp.where(lane == 1, ts[1], 0.0))
+            c_all[b, me] = jnp.where(sub == 0, pair(qs[0], qs[1]), jnp.where(sub == 1, pair(ks[0], ks[1]), jnp.where(sub == 2, taus, 0.0)))
+        for b in range(images):
+            for k in far_first:
+                dst = (me + k) % n
+                rcopy(g_all.at[b, me], g_all.at[b, me], g_s.at[b, k - 1], g_r.at[b, k - 1], dst).start()
+                rcopy(c_all.at[b, me], c_all.at[b, me], c_s.at[b, k - 1], c_r.at[b, k - 1], dst).start()
 
     def gathered(ref, ss, rs, b):
         for k in range(1, n):
@@ -257,8 +283,10 @@
             dot_v[:, pl.ds(off, TOK)] = mm(wo_v[...], dy_v[pl.ds(off, TOK), :], NT).astype(BF16)
             return 0
         lax.fori_loop(0, tiles, body, 0)
+
+    def send_dprobs(b):
         to_pairs(gram(b, dot_v, 0, zt, 2 * dim), ds_out.at[b])
-        for k in range(1, n):
+        for k in far_first:
             dst = (me + k) % n
             rcopy(ds_out.at[b, dst], ds_in.at[b, k - 1], ds_s.at[b, k - 1], ds_r.at[b, k - 1], dst).start()
 
@@ -289,11 +317,17 @@
             r0 = w * wrow
             yield w, r0, min(wrow, dim - r0), min(COLS, dim - r0)
 
-    def out_and_dv(b):
+    def heads_out(b):
         def body(t, _):
             off = pl.multiple_of(b * tokens + t * TOK, TOK)
             for w, r0, m, kk in windows():
                 ot[r0:r0 + m, pl.ds(off, TOK)] = mm(bd[b, w, 0, 0:m, 0:kk], zt[2 * dim + r0:2 * dim + r0 + kk, pl.ds(off, TOK)]).astype(BF16)
+            return 0
+        lax.fori_loop(0, tiles, body, 0)
+
+    def grad_values(b):
+        def body(t, _):
+            off = pl.multiple_of(b * tokens + t * TOK, TOK)
             for w, r0, m, kk in windows():
                 zt[2 * dim + r0:2 * dim + r0 + m, pl.ds(off, TOK)] = mm(bd[b, w, 1, 0:m, 0:kk], dot_v[r0:r0 + kk, pl.ds(off, TOK)]).astype(BF16)
             return 0
@@ -367,17 +401,20 @@
         put_part(c, mm(ut[...], zt[pl.ds(off, COLS), :], NT))
         d2d(c).start()
 
+    values(0)
+    grad_heads(0)
+    send_dprobs(0)
     owner_forward(0)
-    grad_heads(0)
+    values(1)
     owner_forward(1)
     grad_heads(1)
+    send_dprobs(1)
     gathered(a_all, a_s, a_r, 0)
     build(a_all, 0)
-    out_and_dv(0)
+    heads_out(0)
     gathered(a_all, a_s, a_r, 1)
     build(a_all, 1)
-    out_and_dv(1)
-    owner_backward(0)
+    heads_out(1)
     wo_chunk(0, 0)
 
     def wo_loop(c, _):
@@ -385,64 +422,83 @@
         serve1(c - 1)
         return 0
     lax.fori_loop(1, o_chunks, wo_loop, 0)
-    owner_backward(1)
-
-    def v_loop(c, _):
-        qkv_chunk(c, 2 * dim - o_chunks * COLS)
-        serve1(c - 1)
-        return 0
-    lax.fori_loop(o_chunks, 2 * o_chunks, v_loop, 0)
+    owner_backward()
+    serve1(o_chunks - 1)
+    grad_values(0)
+    grad_values(1)
+    v0 = 2 * dim - o_chunks * COLS
+    qkv_chunk(o_chunks, v0)
 
     def s2_body(c, _):
         serve2(c)
         return 0
-    lax.fori_loop(0, o_chunks, s2_body, 0)
+
+    def serve2_range(c0, c1):
+        lax.fori_loop(c0, c1, s2_body, 0)
+
+    serve2_range(0, 2)
+
+    def v_loop(c, _):
+        qkv_chunk(c, v0)
+        serve1(c - 1)
+        return 0
+    lax.fori_loop(o_chunks + 1, 2 * o_chunks, v_loop, 0)
+    serve2_range(2, 3)
     for b in range(images):
         gathered(g_all, g_s, g_r, b)
         gathered(c_all, c_s, c_r, b)
         build(g_all, b)
         dq_and_dk(b)
+        if b == 0:
+            serve1(2 * o_chunks - 1)
+    serve2_range(3, 4)
+    qkv_chunk(2 * o_chunks, -2 * o_chunks * COLS)
 
     def qk_loop(c, _):
         qkv_chunk(c, -2 * o_chunks * COLS)
         serve1(c - 1)
         return 0
-    lax.fori_loop(2 * o_chunks, chunks, qk_loop, 0)
+    lax.fori_loop(2 * o_chunks + 1, chunks, qk_loop, 0)
     serve1(chunks - 1)
-    lax.fori_loop(o_chunks, chunks - 3, s2_body, 0)
-
-    def y_copy(t):
+    serve2_range(4, chunks - 3)
+
+    def tile_copy(i, t):
         b = t // tiles
-        return pltpu.make_async_copy(y_st.at[t], y_hbm.at[b, pl.ds(pl.multiple_of((t % tiles) * TOK, TOK), TOK)], out_sem.at[0, t])
-
-    def dx_copy(t):
-        b = t // tiles
-        return pltpu.make_async_copy(x_v.at[pl.ds(pl.multiple_of(t * TOK, TOK), TOK)], dx_hbm.at[b, pl.ds(pl.multiple_of((t % tiles) * TOK, TOK), TOK)], out_sem.at[1, t])
+        rows = pl.ds(pl.multiple_of(t * TOK, TOK), TOK)
+        out_rows = pl.ds(pl.multiple_of((t % tiles) * TOK, TOK), TOK)
+        src, dst = ((x_v, y_hbm), (dy_v, dx_hbm))[i]
+        return pltpu.make_async_copy(src.at[rows], dst.at[b, out_rows], out_sem.at[i, t])
+
+    def dx_body(t, _):
+        off = pl.multiple_of(t * TOK, TOK)
+        dot_v[:, pl.ds(off, TOK)] = mm(w_v[...], zt[:, pl.ds(off, TOK)]).astype(BF16)
+
+        def piece(i, _):
+            r = pl.ds(pl.multiple_of(off + i * LANES, LANES), LANES)
+            du = dot_v[:, r].T.astype(F32)
+            x_hat, inv = norm(x_v[r, :].astype(F32))
+            prod = du * x_hat
+            dgb[0] += jnp.sum(prod.reshape(LANES // 8, 8, dim), axis=0)
+            dgb[1] += jnp.sum(du.reshape(LANES // 8, 8, dim), axis=0)
+            a9 = du * gain_row
+            m1 = jnp.sum(a9, axis=-1, keepdims=True) * (1.0 / dim)
+            m2 = jnp.sum(a9 * x_hat, axis=-1, keepdims=True) * (1.0 / dim)
+            gx = inv * (a9 - m1 - x_hat * m2)
+            dy_v[r, :] = (dy_v[r, :].astype(F32) + gx).astype(BF16)
+            return 0
+        lax.fori_loop(0, TOK // LANES, piece, 0)
+        tile_copy(1, t).start()
+        return 0
 
     def y_body(t, _):
         off = pl.multiple_of(t * TOK, TOK)
-        o = ot[:, pl.ds(off, TOK)].T
-        y_st[t] = (x_v[pl.ds(off, TOK), :].astype(F32) + mm(o, wo_v[...])).astype(BF16)
-        y_copy(t).start()
-        return 0
+        x_v[pl.ds(off, TOK), :] = (x_v[pl.ds(off, TOK), :].astype(F32) + mm(ot[:, pl.ds(off, TOK)].T, wo_v[...])).astype(BF16)
+        tile_copy(0, t).start()
+        return 0
+    lax.fori_loop(0, 1, dx_body, 0)
+    serve2_range(chunks - 3, chunks)
+    lax.fori_loop(1, images * tiles, dx_body, 0)
     lax.fori_loop(0, images * tiles, y_body, 0)
-    lax.fori_loop(chunks - 3, chunks, s2_body, 0)
-
-    def dx_body(t, _):
-        off = pl.multiple_of(t * TOK, TOK)
-        du = mm(w_v[...], zt[:, pl.ds(off, TOK)]).astype(BF16).T.astype(F32)
-        x_hat, inv = norm(x_v[pl.ds(off, TOK), :].astype(F32))
-        prod = du * x_hat
-        dgb[0] += jnp.sum(prod.reshape(TOK // 8, 8, dim), axis=0)
-        dgb[1] += jnp.sum(du.reshape(TOK // 8, 8, dim), axis=0)
-        a9 = du * gain_row
-        m1 = jnp.sum(a9, axis=-1, keepdims=True) * (1.0 / dim)
-        m2 = jnp.sum(a9 * x_hat, axis=-1, keepdims=True) * (1.0 / dim)
-        gx = inv * (a9 - m1 - x_hat * m2)
-        x_v[pl.ds(off, TOK), :] = (dy_v[pl.ds(off, TOK), :].astype(F32) + gx).astype(BF16)
-        dx_copy(t).start()
-        return 0
-    lax.fori_loop(0, images * tiles, dx_body, 0)
 
     sub8 = lax.broadcasted_iota(jnp.int32, (8, dim), 0)
     gb = jnp.where(sub8 == 0, jnp.sum(dgb[0], axis=0, keepdims=True), jnp.where(sub8 == 1, jnp.sum(dgb[1], axis=0, keepdims=True), 0.0))
@@ -504,10 +560,38 @@
     lax.fori_loop(0, chunks, drain, 0)
 
     def drain_out(t, _):
-        y_copy(t).wait()
-        dx_copy(t).wait()
+        tile_copy(0, t).wait()
+        tile_copy(1, t).wait()
         return 0
     lax.fori_loop(0, images * tiles, drain_out, 0)
+
+
+def finish_kernel(heads, y_hbm, dx_hbm, dwqkv_hbm, dwo_hbm, dgain_ref, dbias_ref, dtau_ref,
+                  y_out, dx_out, dwqkv_out, dwo_out, dgain_out, dbias_out, dtau_out,
+                  buf, q_buf, o_buf, sem_in, sem_out):
+    images, tokens, dim = y_hbm.shape
+    parts = tokens // TOK
+    moves = []
+    for a, (src, dst) in enumerate(((y_hbm, y_out), (dx_hbm, dx_out))):
+        for b in range(images):
+            for t in range(parts):
+                i = len(moves)
+                rows = pl.ds(t * TOK, TOK)
+                moves.append((src.at[b, rows], buf.at[i], dst.at[b, rows]))
+    moves.append((dwqkv_hbm, q_buf, dwqkv_out))
+    moves.append((dwo_hbm, o_buf, dwo_out))
+    ins = [pltpu.make_async_copy(s, v, sem_in.at[i]) for i, (s, v, _d) in enumerate(moves)]
+    outs = [pltpu.make_async_copy(v, d, sem_out.at[i]) for i, (_s, v, d) in enumerate(moves)]
+    for c in ins:
+        c.start()
+    dgain_out[...] = dgain_ref[...].reshape(dgain_out.shape)
+    dbias_out[...] = dbias_ref[...].reshape(dbias_out.shape)
+    dtau_out[...] = dtau_ref[...].reshape(dtau_ref.shape[1])[:heads]
+    for c, o in zip(ins, outs):
+        c.wait()
+        o.start()
+    for o in outs:
+        o.wait()
 
 
 def solution(mesh):
@@ -523,7 +607,6 @@
         nwin = -(-heads // (COLS // hd))
         any_spec = pl.BlockSpec(memory_space=pl.ANY)
         vmem = pl.BlockSpec(memory_space=pltpu.VMEM)
-        smem = pl.BlockSpec(memory_space=pltpu.SMEM)
         dma = pltpu.SemaphoreType.DMA
         pairs = (images, n - 1)
         out = pl.pallas_call(
@@ -537,9 +620,12 @@
                 jax.ShapeDtypeStruct((1, dim), F32),
                 jax.ShapeDtypeStruct((1, LANES), F32),
             ),
-            in_specs=[any_spec, any_spec, vmem, vmem, any_spec, any_spec, smem],
+            in_specs=[any_spec] * 7,
             out_specs=(any_spec, any_spec, vmem, vmem, vmem, vmem, vmem),
             scratch_shapes=[
+                pltpu.VMEM((dim,), F32),
+                pltpu.VMEM((dim,), F32),
+                pltpu.VMEM((heads,), F32),
                 pltpu.VMEM((rows, dim), BF16),
                 pltpu.VMEM((rows, dim), BF16),
                 pltpu.VMEM((dim, 3 * dim), BF16),
@@ -549,11 +635,10 @@
                 pltpu.VMEM((3 * dim, rows), BF16),
                 pltpu.VMEM((dim, rows), BF16),
                 pltpu.VMEM((dim, rows), BF16),
-                pltpu.VMEM((rows // TOK, TOK, dim), BF16),
-                pltpu.VMEM((images, 2, dim, LANES), F32),
-                pltpu.VMEM((images, n, hd + 8, LANES), F32),
-                pltpu.VMEM((images, n - 1, hd + 8, LANES), F32),
-                pltpu.VMEM((images, hd + 8, LANES), F32),
+                pltpu.VMEM((images, 2 * dim, LANES), F32),
+                pltpu.VMEM((images, n, hd, LANES), F32),
+                pltpu.VMEM((images, n - 1, hd, LANES), F32),
+                pltpu.VMEM((images, hd, LANES), F32),
                 pltpu.VMEM((images, n, hd, LANES), BF16),
                 pltpu.VMEM((images, n, hd, LANES), F32),
                 pltpu.VMEM((images, n - 1, hd, LANES), F32),
@@ -563,13 +648,12 @@
                 pltpu.VMEM((dim, LANES), F32),
                 pltpu.VMEM((dim, LANES), F32),
                 pltpu.VMEM((2, 8, dim), F32),
-                pltpu.VMEM((8, dim), F32),
                 pltpu.VMEM((n, 8, dim), F32),
                 pltpu.VMEM((chunks, 2, n // 2, per_dev, COLS), F32),
                 pltpu.VMEM((chunks, n // 2, per_dev, COLS), F32),
                 pltpu.VMEM((chunks, 2, per_dev // 2, COLS), F32),
                 pltpu.VMEM((chunks, 2, per_dev, COLS), F32),
-                dma((6,)), dma((2, rows // TOK)),
+                dma((rows // TOK + images + 6,)), dma((2, rows // TOK)),
                 dma((chunks,)), dma((chunks,)),
                 dma((chunks, 2)), dma((chunks, 2)), dma((chunks, 2)), dma((chunks, 2)),
                 dma(pairs), dma(pairs), dma(pairs), dma(pairs), dma(pairs), dma(pairs),
@@ -579,9 +663,29 @@
             compiler_params=pltpu.CompilerParams(
                 collective_id=0, has_side_effects=True, vmem_limit_bytes=67043328),
             name="xca_block",
-        )(x_in, grad_y, ln_gain.reshape(1, dim), ln_bias.reshape(1, dim), w_qkv, w_out, temp_tau)
-        y, dx, dwqkv, dwo, dgain, dbias, dtau = out
-        return y, dx, dwqkv, dwo, dgain.reshape(dim), dbias.reshape(dim), dtau[0, :heads]
+        )(x_in, grad_y, ln_gain, ln_bias, w_qkv, w_out, temp_tau)
+        moves = 2 * rows // TOK + 2
+        return pl.pallas_call(
+            functools.partial(finish_kernel, heads),
+            out_shape=(
+                jax.ShapeDtypeStruct(x_in.shape, BF16),
+                jax.ShapeDtypeStruct(x_in.shape, BF16),
+                jax.ShapeDtypeStruct((per_dev, 3 * dim), BF16),
+                jax.ShapeDtypeStruct((per_dev, dim), BF16),
+                jax.ShapeDtypeStruct((dim,), F32),
+                jax.ShapeDtypeStruct((dim,), F32),
+                jax.ShapeDtypeStruct((heads,), F32),
+            ),
+            in_specs=[any_spec] * 4 + [vmem] * 3,
+            out_specs=(any_spec,) * 4 + (vmem,) * 3,
+            scratch_shapes=[
+                pltpu.VMEM((2 * rows // TOK, TOK, dim), BF16),
+                pltpu.VMEM((per_dev, 3 * dim), BF16),
+                pltpu.VMEM((per_dev, dim), BF16),
+                dma((moves,)), dma((moves,)),
+            ],
+            name="finish",
+        )(*out)
 
     tok = P("dp", "sp", None)
     return jax.shard_map(

time: 95.7 us -> 86.6 us (0.905)
  local copies, waits for them, and re-layouts: 10.7 us -> 0 us
  Pallas kernels: 81.5 us -> 85.6 us
  other arithmetic: 2.56 us -> 0 us
    unnamed x10 -> x0, local copies, waits for them, and re-layouts: 7 us -> none
    pallas_call x0 -> x1, Pallas kernels: none -> 6.96 us  [local_step(): pl.pallas_call(functools.partial(finish_kernel, heads), out_shape=(jax.Sh...]
    pallas_call x1, Pallas kernels: 81.5 us -> 78.7 us  [local_step(): pl.pallas_call(functools.partial(xca_kernel, n, heads), out_shape=(jax.Sh...]
    pallas_call x2 -> x0, other arithmetic: 2.56 us -> none  [local_step(): pl.pallas_call(functools.partial(xca_kernel, n, heads), out_shape=(jax.Sh...]
    reshape x2 -> x0, local copies, waits for them, and re-layouts: 2.53 us -> none  [the longest x1 1.27 us: local_step(): ln_gain.reshape(1, dim)]
    squeeze x1 -> x0, local copies, waits for them, and re-layouts: 1.17 us -> none  [local_step(): dtau[0, :heads]]
where the time goes in v1:
time: 86.6 us; the launch traced here: 86.4 us
  Pallas kernels  85.6 us (99%)
    pallas_call x1, Pallas kernels, local_step(): pl.pallas_call(functools.partial(xca_kernel, n, heads), out_shape=(jax.Sh...  78.7 us
    pallas_call x1, Pallas kernels, local_step(): pl.pallas_call(functools.partial(finish_kernel, heads), out_shape=(jax.Sh...  6.96 us

profile of v1, /device:TPU:113, one launch (start us, length us, event | category | flops | bytes accessed | tf_op | source)
XLA Modules:
  0.0 86.4 jit_solution(237645552822519875)
XLA Ops:
  0.6 78.7 %xca_block.1 = (bf16[2,1024,768]{2,1,0:T(8,128)(2,1)}, bf16[2,1024,768]{2,1,0:T(8,128)(2,1)}, bf16[96,2304]{1,0:T(8,128)(2,1)}, bf16[96,768]{1,0:T(8,128)(2,1)},...) custom-call(bf16[2,1024,768]{2,1,0:T(8,128)(2,1)} %x_hbm.1, bf16[2,1024,768]{2,1,0:T(8,128)(2,1)} %dy_hbm.1, ...), custom_call_target="tpu_custom_call" | custom-call | tf_op jit(solution)/shard_map/xca_block/pallas_call | solution.py:612
  79.3 7.0 %finish.1 = (bf16[2,1024,768]{2,1,0:T(8,128)(2,1)}, bf16[2,1024,768]{2,1,0:T(8,128)(2,1)}, bf16[96,2304]{1,0:T(8,128)(2,1)}, bf16[96,768]{1,0:T(8,128)(2,1)}, f3...) custom-call(bf16[2,1024,768]{2,1,0:T(8,128)(2,1)} %get-tuple-element.14.y_hbm, bf16[2,1024,768]{2,1,0:T(8,128)(2,1)} %get-tuple-element.15.dx_hbm, ...), custom_call_target="tpu_custom_call" | custom-call | tf_op jit(solution)/shard_map/finish/pallas_call | solution.py:668

commit v2 on v1

--- a/solution.py
+++ b/solution.py
@@ -13,6 +13,7 @@
 LANES = 128
 TOK = 512
 COLS = 256
+VMEM_LIMIT = 67043328
 NN = (((1,), (0,)), ((), ()))
 NT = (((1,), (1,)), ((), ()))
 
@@ -49,7 +50,8 @@
     partner = chip * 2 + (1 - core)
     cr, cl, co = (chip + 1) % chips, (chip + chips - 1) % chips, (chip + 2) % chips
 
-    far_first = sorted(range(1, n), key=lambda k: abs(2 * k - n))
+    peers = range(1, n)
+    far_first = sorted(peers, key=lambda k: abs(2 * k - n))
 
     def rcopy(src, dst, ss, rs, dev):
         return pltpu.make_async_remote_copy(
@@ -76,7 +78,7 @@
     cp_x(0, 1).start()
 
     barrier = pltpu.get_barrier_semaphore()
-    for k in range(1, n):
+    for k in peers:
         pl.semaphore_signal(barrier, inc=1, device_id={"sp": (me + k) % n},
                             device_id_type=pl.DeviceIdType.MESH)
     sq_acc[...] = jnp.zeros_like(sq_acc)
@@ -162,14 +164,14 @@
             pl.semaphore_wait(barrier, n - 1)
         for k in far_first:
             dst = (me + k) % n
-            rcopy(gs_out.at[b, dst], gs_in.at[b, k - 1], gs_s.at[b, k - 1], gs_r.at[b, k - 1], dst).start()
-
+            rcopy(gs_out.at[b, dst], gs_in.at[b, k], gs_s.at[b, k], gs_r.at[b, k], dst).start()
+
+    for b in range(1, images):
+        for t in range(tiles):
+            cp_x(b, t).start()
     norm_rows(0, TOK)
     cp_x(0, 1).wait()
     cp_wqk.wait()
-    for b in range(1, images):
-        for t in range(tiles):
-            cp_x(b, t).start()
     cp_wv.start()
     cp_wo.start()
     for b in range(images):
@@ -192,11 +194,9 @@
     send_gram(1)
 
     def values(b):
-        def v_body(t, _):
-            off = pl.multiple_of(b * tokens + t * TOK, TOK)
-            zt[2 * dim:3 * dim, pl.ds(off, TOK)] = mm(wt_v[2 * dim:3 * dim, :], ut[:, pl.ds(off, TOK)]).astype(BF16)
-            return 0
-        lax.fori_loop(0, tiles, v_body, 0)
+        for t in range(tiles):
+            tok_t = pl.ds(b * tokens + t * TOK, TOK)
+            zt[2 * dim:3 * dim, tok_t] = mm(wt_v[2 * dim:3 * dim, :], ut[:, tok_t]).astype(BF16)
 
     eye = lax.broadcasted_iota(jnp.int32, (hd, hd), 0) == lax.broadcasted_iota(jnp.int32, (hd, hd), 1)
 
@@ -225,29 +225,29 @@
         return jnp.concatenate([a0, a1, z], axis=1)
 
     def owner_forward(b):
-        for k in range(1, n):
-            rcopy(gs_out.at[b, 0], gs_in.at[b, k - 1], gs_s.at[b, k - 1], gs_r.at[b, k - 1], me).wait_recv()
+        for k in peers:
+            rcopy(gs_out.at[b, 0], gs_in.at[b, k], gs_s.at[b, k], gs_r.at[b, k], me).wait_recv()
         tot = gs_out[b, me]
-        for k in range(1, n):
-            tot = tot + gs_in[b, k - 1]
+        for k in peers:
+            tot = tot + gs_in[b, k]
         gs_sum[b] = tot
         p0 = attn_state(b, 0)[2]
         p1 = attn_state(b, 1)[2]
         a_all[b, me] = pair(p0, p1).astype(BF16)
         for k in far_first:
             dst = (me + k) % n
-            rcopy(a_all.at[b, me], a_all.at[b, me], a_s.at[b, k - 1], a_r.at[b, k - 1], dst).start()
+            rcopy(a_all.at[b, me], a_all.at[b, me], a_s.at[b, k], a_r.at[b, k], dst).start()
 
     def owner_backward():
         for b in range(images):
-            for k in range(1, n):
-                rcopy(ds_out.at[b, 0], ds_in.at[b, k - 1], ds_s.at[b, k - 1], ds_r.at[b, k - 1], me).wait_recv()
+            for k in peers:
+                rcopy(ds_out.at[b, 0], ds_in.at[b, k], ds_s.at[b, k], ds_r.at[b, k], me).wait_recv()
         sub = lax.broadcasted_iota(jnp.int32, (8, LANES), 0)
         lane = lax.broadcasted_iota(jnp.int32, (8, LANES), 1)
         for b in range(images):
             tot = ds_out[b, me]
-            for k in range(1, n):
-                tot = tot + ds_in[b, k - 1]
+            for k in peers:
+                tot = tot + ds_in[b, k]
             tot = tot.astype(BF16).astype(F32)
             gs, qs, ks, ts = [], [], [], []
             for s in range(2):
@@ -265,30 +265,28 @@
         for b in range(images):
             for k in far_first:
                 dst = (me + k) % n
-                rcopy(g_all.at[b, me], g_all.at[b, me], g_s.at[b, k - 1], g_r.at[b, k - 1], dst).start()
-                rcopy(c_all.at[b, me], c_all.at[b, me], c_s.at[b, k - 1], c_r.at[b, k - 1], dst).start()
+                rcopy(g_all.at[b, me], g_all.at[b, me], g_s.at[b, k], g_r.at[b, k], dst).start()
+                rcopy(c_all.at[b, me], c_all.at[b, me], c_s.at[b, k], c_r.at[b, k], dst).start()
 
     def gathered(ref, ss, rs, b):
-        for k in range(1, n):
+        for k in peers:
             src = (me + n - k) % n
-            rcopy(ref.at[b, me], ref.at[b, src], ss.at[b, k - 1], rs.at[b, k - 1], me).wait_recv()
+            rcopy(ref.at[b, me], ref.at[b, src], ss.at[b, k], rs.at[b, k], me).wait_recv()
 
     def grad_heads(b):
         cp_dy(b).wait()
         if b == 0:
             cp_wo.wait()
 
-        def body(t, _):
-            off = pl.multiple_of(b * tokens + t * TOK, TOK)
-            dot_v[:, pl.ds(off, TOK)] = mm(wo_v[...], dy_v[pl.ds(off, TOK), :], NT).astype(BF16)
-            return 0
-        lax.fori_loop(0, tiles, body, 0)
+        for t in range(tiles):
+            tok_t = pl.ds(b * tokens + t * TOK, TOK)
+            dot_v[:, tok_t] = mm(wo_v[...], dy_v[tok_t, :], NT).astype(BF16)
 
     def send_dprobs(b):
         to_pairs(gram(b, dot_v, 0, zt, 2 * dim), ds_out.at[b])
         for k in far_first:
             dst = (me + k) % n
-            rcopy(ds_out.at[b, dst], ds_in.at[b, k - 1], ds_s.at[b, k - 1], ds_r.at[b, k - 1], dst).start()
+            rcopy(ds_out.at[b, dst], ds_in.at[b, k], ds_s.at[b, k], ds_r.at[b, k], dst).start()
 
     sj = lax.broadcasted_iota(jnp.int32, (LANES, COLS), 0)
     slane = lax.broadcasted_iota(jnp.int32, (LANES, COLS), 1)
@@ -318,12 +316,10 @@
             yield w, r0, min(wrow, dim - r0), min(COLS, dim - r0)
 
     def heads_out(b):
-        def body(t, _):
-            off = pl.multiple_of(b * tokens + t * TOK, TOK)
+        for t in range(tiles):
+            tok_t = pl.ds(b * tokens + t * TOK, TOK)
             for w, r0, m, kk in windows():
-                ot[r0:r0 + m, pl.ds(off, TOK)] = mm(bd[b, w, 0, 0:m, 0:kk], zt[2 * dim + r0:2 * dim + r0 + kk, pl.ds(off, TOK)]).astype(BF16)
-            return 0
-        lax.fori_loop(0, tiles, body, 0)
+                ot[r0:r0 + m, tok_t] = mm(bd[b, w, 0, 0:m, 0:kk], zt[2 * dim + r0:2 * dim + r0 + kk, tok_t]).astype(BF16)
 
     def grad_values(b):
         def body(t, _):
@@ -353,9 +349,12 @@
             return 0
         lax.fori_loop(0, tiles, body, 0)
 
-    def put_part(c, val):
+    def put_part(c, val, more=False):
         for j in range(n):
-            part[c, j % 2, j // 2] = val[j * per_dev:(j + 1) * per_dev, :]
+            rows_j = val[j * per_dev:(j + 1) * per_dev, :]
+            if more:
+                rows_j += part[c, j % 2, j // 2]
+            part[c, j % 2, j // 2] = rows_j
 
     def d2d(c):
         return rcopy(part.at[c, 1 - core], r1.at[c], d2d_s.at[c], d2d_r.at[c], partner)
@@ -390,11 +389,12 @@
             h.wait_recv()
         return (r1[c, chip] + r3[c, 0] + r3[c, 1]).astype(BF16)
 
-    def wo_chunk(c, _):
+    def wo_chunk(c, b):
         off = pl.multiple_of(c * COLS, COLS)
-        put_part(c, mm(ot[...], dy_v[:, pl.ds(off, COLS)]))
-        d2d(c).start()
-        return 0
+        tok_b = slice(b * tokens, (b + 1) * tokens)
+        put_part(c, mm(ot[:, tok_b], dy_v[tok_b, pl.ds(off, COLS)]), b > 0)
+        if b + 1 == images:
+            d2d(c).start()
 
     def qkv_chunk(c, base):
         off = pl.multiple_of(base + c * COLS, COLS)
@@ -403,25 +403,21 @@
 
     values(0)
     grad_heads(0)
+    owner_forward(0)
     send_dprobs(0)
-    owner_forward(0)
     values(1)
     owner_forward(1)
     grad_heads(1)
     send_dprobs(1)
-    gathered(a_all, a_s, a_r, 0)
-    build(a_all, 0)
-    heads_out(0)
-    gathered(a_all, a_s, a_r, 1)
-    build(a_all, 1)
-    heads_out(1)
-    wo_chunk(0, 0)
-
-    def wo_loop(c, _):
-        wo_chunk(c, 0)
-        serve1(c - 1)
-        return 0
-    lax.fori_loop(1, o_chunks, wo_loop, 0)
+    for b in range(images):
+        gathered(a_all, a_s, a_r, b)
+        build(a_all, b)
+        heads_out(b)
+
+        for c in range(o_chunks):
+            wo_chunk(c, b)
+            if b + 1 == images and c > 0:
+                serve1(c - 1)
     owner_backward()
     serve1(o_chunks - 1)
     grad_values(0)
@@ -463,11 +459,9 @@
     serve2_range(4, chunks - 3)
 
     def tile_copy(i, t):
-        b = t // tiles
-        rows = pl.ds(pl.multiple_of(t * TOK, TOK), TOK)
-        out_rows = pl.ds(pl.multiple_of((t % tiles) * TOK, TOK), TOK)
+        rows_t = pl.ds(pl.multiple_of(t * TOK, TOK), TOK)
         src, dst = ((x_v, y_hbm), (dy_v, dx_hbm))[i]
-        return pltpu.make_async_copy(src.at[rows], dst.at[b, out_rows], out_sem.at[i, t])
+        return pltpu.make_async_copy(src.at[rows_t], dst.at[rows_t], out_sem.at[i, t])
 
     def dx_body(t, _):
         off = pl.multiple_of(t * TOK, TOK)
@@ -498,14 +492,10 @@
     lax.fori_loop(0, 1, dx_body, 0)
     serve2_range(chunks - 3, chunks)
     lax.fori_loop(1, images * tiles, dx_body, 0)
+    gb_all[me] = jnp.concatenate([jnp.sum(dgb[i], axis=0).reshape(dim // LANES, LANES) for i in range(2)], axis=0)
+    for k in far_first:
+        rcopy(gb_all.at[me], gb_all.at[me], gb_s.at[k], gb_r.at[k], (me + k) % n).start()
     lax.fori_loop(0, images * tiles, y_body, 0)
-
-    sub8 = lax.broadcasted_iota(jnp.int32, (8, dim), 0)
-    gb = jnp.where(sub8 == 0, jnp.sum(dgb[0], axis=0, keepdims=True), jnp.where(sub8 == 1, jnp.sum(dgb[1], axis=0, keepdims=True), 0.0))
-    gb_all[me] = gb
-    for k in range(1, n):
-        dst = (me + k) % n
-        rcopy(gb_all.at[me], gb_all.at[me], gb_s.at[k - 1], gb_r.at[k - 1], dst).start()
 
     lane = lax.broadcasted_iota(jnp.int32, (1, LANES), 1)
     dtau = jnp.zeros((1, LANES), F32)
@@ -528,14 +518,14 @@
         return 0
     lax.fori_loop(o_chunks, 2 * o_chunks, s3_v, 0)
 
-    for k in range(1, n):
+    for k in peers:
         src = (me + n - k) % n
-        rcopy(gb_all.at[me], gb_all.at[src], gb_s.at[k - 1], gb_r.at[k - 1], me).wait_recv()
+        rcopy(gb_all.at[me], gb_all.at[src], gb_s.at[k], gb_r.at[k], me).wait_recv()
     tot = gb_all[0]
     for d in range(1, n):
         tot = tot + gb_all[d]
-    dgain_ref[...] = tot[0:1, :]
-    dbias_ref[...] = tot[1:2, :]
+    dgain_ref[...] = tot[:dim // LANES]
+    dbias_ref[...] = tot[dim // LANES:]
 
     def s3_qk(c, _):
         dwqkv_ref[:, pl.ds(pl.multiple_of(c * COLS - 2 * dim, COLS), COLS)] = serve3(c)
@@ -543,14 +533,14 @@
     lax.fori_loop(2 * o_chunks, chunks, s3_qk, 0)
 
     for b in range(images):
-        for k in range(1, n):
-            rcopy(gs_out.at[b, 0], gs_in.at[b, k - 1], gs_s.at[b, k - 1], gs_r.at[b, k - 1], me).wait_send()
-            rcopy(a_all.at[b, me], a_all.at[b, me], a_s.at[b, k - 1], a_r.at[b, k - 1], me).wait_send()
-            rcopy(ds_out.at[b, 0], ds_in.at[b, k - 1], ds_s.at[b, k - 1], ds_r.at[b, k - 1], me).wait_send()
-            rcopy(g_all.at[b, me], g_all.at[b, me], g_s.at[b, k - 1], g_r.at[b, k - 1], me).wait_send()
-            rcopy(c_all.at[b, me], c_all.at[b, me], c_s.at[b, k - 1], c_r.at[b, k - 1], me).wait_send()
-    for k in range(1, n):
-        rcopy(gb_all.at[me], gb_all.at[me], gb_s.at[k - 1], gb_r.at[k - 1], me).wait_send()
+        for k in peers:
+            rcopy(gs_out.at[b, 0], gs_in.at[b, k], gs_s.at[b, k], gs_r.at[b, k], me).wait_send()
+            rcopy(a_all.at[b, me], a_all.at[b, me], a_s.at[b, k], a_r.at[b, k], me).wait_send()
+            rcopy(ds_out.at[b, 0], ds_in.at[b, k], ds_s.at[b, k], ds_r.at[b, k], me).wait_send()
+            rcopy(g_all.at[b, me], g_all.at[b, me], g_s.at[b, k], g_r.at[b, k], me).wait_send()
+            rcopy(c_all.at[b, me], c_all.at[b, me], c_s.at[b, k], c_r.at[b, k], me).wait_send()
+    for k in peers:
+        rcopy(gb_all.at[me], gb_all.at[me], gb_s.at[k], gb_r.at[k], me).wait_send()
 
     def drain(c, _):
         d2d(c).wait_send()
@@ -558,32 +548,26 @@
             h.wait_send()
         return 0
     lax.fori_loop(0, chunks, drain, 0)
-
-    def drain_out(t, _):
-        tile_copy(0, t).wait()
-        tile_copy(1, t).wait()
-        return 0
-    lax.fori_loop(0, images * tiles, drain_out, 0)
-
-
-def finish_kernel(heads, y_hbm, dx_hbm, dwqkv_hbm, dwo_hbm, dgain_ref, dbias_ref, dtau_ref,
-                  y_out, dx_out, dwqkv_out, dwo_out, dgain_out, dbias_out, dtau_out,
-                  buf, q_buf, o_buf, sem_in, sem_out):
-    images, tokens, dim = y_hbm.shape
+    for i in range(2):
+        for t in range(images * tiles):
+            tile_copy(i, t).wait()
+
+
+def finish_kernel(heads, y_hbm, dx_hbm, dwqkv_ref, dwo_ref, dgain_ref, dbias_ref, dtau_ref,
+                  y_out, dx_out, dwqkv_out, dwo_out, dgain_out, dbias_out, dtau_out, buf, sem_in, sem_out):
+    images, tokens, dim = y_out.shape
     parts = tokens // TOK
-    moves = []
-    for a, (src, dst) in enumerate(((y_hbm, y_out), (dx_hbm, dx_out))):
+    ins, outs = [], []
+    for src, dst in ((y_hbm, y_out), (dx_hbm, dx_out)):
         for b in range(images):
             for t in range(parts):
-                i = len(moves)
-                rows = pl.ds(t * TOK, TOK)
-                moves.append((src.at[b, rows], buf.at[i], dst.at[b, rows]))
-    moves.append((dwqkv_hbm, q_buf, dwqkv_out))
-    moves.append((dwo_hbm, o_buf, dwo_out))
-    ins = [pltpu.make_async_copy(s, v, sem_in.at[i]) for i, (s, v, _d) in enumerate(moves)]
-    outs = [pltpu.make_async_copy(v, d, sem_out.at[i]) for i, (_s, v, d) in enumerate(moves)]
+                i = len(ins)
+                ins.append(pltpu.make_async_copy(src.at[pl.ds((b * parts + t) * TOK, TOK)], buf.at[i], sem_in.at[i]))
+                outs.append(pltpu.make_async_copy(buf.at[i], dst.at[b, pl.ds(t * TOK, TOK)], sem_out.at[i]))
     for c in ins:
         c.start()
+    dwqkv_out[...] = dwqkv_ref[...]
+    dwo_out[...] = dwo_ref[...]
     dgain_out[...] = dgain_ref[...].reshape(dgain_out.shape)
     dbias_out[...] = dbias_ref[...].reshape(dbias_out.shape)
     dtau_out[...] = dtau_ref[...].reshape(dtau_ref.shape[1])[:heads]
@@ -608,20 +592,20 @@
         any_spec = pl.BlockSpec(memory_space=pl.ANY)
         vmem = pl.BlockSpec(memory_space=pltpu.VMEM)
         dma = pltpu.SemaphoreType.DMA
-        pairs = (images, n - 1)
+        pairs = (images, n)
         out = pl.pallas_call(
             functools.partial(xca_kernel, n, heads),
             out_shape=(
-                jax.ShapeDtypeStruct(x_in.shape, BF16),
-                jax.ShapeDtypeStruct(x_in.shape, BF16),
+                jax.ShapeDtypeStruct((rows, dim), BF16),
+                jax.ShapeDtypeStruct((rows, dim), BF16),
                 jax.ShapeDtypeStruct((per_dev, 3 * dim), BF16),
                 jax.ShapeDtypeStruct((per_dev, dim), BF16),
-                jax.ShapeDtypeStruct((1, dim), F32),
-                jax.ShapeDtypeStruct((1, dim), F32),
+                jax.ShapeDtypeStruct((dim // LANES, LANES), F32),
+                jax.ShapeDtypeStruct((dim // LANES, LANES), F32),
                 jax.ShapeDtypeStruct((1, LANES), F32),
             ),
             in_specs=[any_spec] * 7,
-            out_specs=(any_spec, any_spec, vmem, vmem, vmem, vmem, vmem),
+            out_specs=(any_spec,) * 2 + (vmem,) * 5,
             scratch_shapes=[
                 pltpu.VMEM((dim,), F32),
                 pltpu.VMEM((dim,), F32),
@@ -637,18 +621,18 @@
                 pltpu.VMEM((dim, rows), BF16),
                 pltpu.VMEM((images, 2 * dim, LANES), F32),
                 pltpu.VMEM((images, n, hd, LANES), F32),
-                pltpu.VMEM((images, n - 1, hd, LANES), F32),
+                pltpu.VMEM((images, n, hd, LANES), F32),
                 pltpu.VMEM((images, hd, LANES), F32),
                 pltpu.VMEM((images, n, hd, LANES), BF16),
                 pltpu.VMEM((images, n, hd, LANES), F32),
-                pltpu.VMEM((images, n - 1, hd, LANES), F32),
+                pltpu.VMEM((images, n, hd, LANES), F32),
                 pltpu.VMEM((images, n, hd, LANES), BF16),
                 pltpu.VMEM((images, n, 8, LANES), F32),
                 pltpu.VMEM((images, nwin, 2, COLS, COLS), BF16),
                 pltpu.VMEM((dim, LANES), F32),
                 pltpu.VMEM((dim, LANES), F32),
                 pltpu.VMEM((2, 8, dim), F32),
-                pltpu.VMEM((n, 8, dim), F32),
+                pltpu.VMEM((n, 2 * dim // LANES, LANES), F32),
                 pltpu.VMEM((chunks, 2, n // 2, per_dev, COLS), F32),
                 pltpu.VMEM((chunks, n // 2, per_dev, COLS), F32),
                 pltpu.VMEM((chunks, 2, per_dev // 2, COLS), F32),
@@ -658,13 +642,12 @@
                 dma((chunks, 2)), dma((chunks, 2)), dma((chunks, 2)), dma((chunks, 2)),
                 dma(pairs), dma(pairs), dma(pairs), dma(pairs), dma(pairs), dma(pairs),
                 dma(pairs), dma(pairs), dma(pairs), dma(pairs),
-                dma((n - 1,)), dma((n - 1,)),
+                dma((n,)), dma((n,)),
             ],
             compiler_params=pltpu.CompilerParams(
-                collective_id=0, has_side_effects=True, vmem_limit_bytes=67043328),
+                collective_id=0, has_side_effects=True, vmem_limit_bytes=VMEM_LIMIT),
             name="xca_block",
         )(x_in, grad_y, ln_gain, ln_bias, w_qkv, w_out, temp_tau)
-        moves = 2 * rows // TOK + 2
         return pl.pallas_call(
             functools.partial(finish_kernel, heads),
             out_shape=(
@@ -676,13 +659,11 @@
                 jax.ShapeDtypeStruct((dim,), F32),
                 jax.ShapeDtypeStruct((heads,), F32),
             ),
-            in_specs=[any_spec] * 4 + [vmem] * 3,
-            out_specs=(any_spec,) * 4 + (vmem,) * 3,
+            in_specs=[any_spec] * 2 + [vmem] * 5,
+            out_specs=(any_spec,) * 2 + (vmem,) * 5,
             scratch_shapes=[
                 pltpu.VMEM((2 * rows // TOK, TOK, dim), BF16),
-                pltpu.VMEM((per_dev, 3 * dim), BF16),
-                pltpu.VMEM((per_dev, dim), BF16),
-                dma((moves,)), dma((moves,)),
+                dma((2 * rows // TOK,)), dma((2 * rows // TOK,)),
             ],
             name="finish",
         )(*out)

time: 86.6 us -> 84.4 us (0.975)
  Pallas kernels: 85.6 us -> 83.5 us
    pallas_call x1, Pallas kernels: 78.7 us -> 76.1 us  [local_step(): pl.pallas_call(functools.partial(xca_kernel, n, heads), out_shape=(jax.Sh...]
where the time goes in v2:
time: 84.4 us; the launch traced here: 84.3 us
  Pallas kernels  83.5 us (99%)
    pallas_call x1, Pallas kernels, local_step(): pl.pallas_call(functools.partial(xca_kernel, n, heads), out_shape=(jax.Sh...  76.1 us
    pallas_call x1, Pallas kernels, local_step(): pl.pallas_call(functools.partial(finish_kernel, heads), out_shape=(jax.Sh...  7.44 us

profile of v2, /device:TPU:113, one launch (start us, length us, event | category | flops | bytes accessed | tf_op | source)
XLA Modules:
  0.0 84.3 jit_solution(1377468912769669190)
XLA Ops:
  0.6 76.1 %xca_block.1 = (bf16[2048,768]{1,0:T(8,128)(2,1)}, bf16[2048,768]{1,0:T(8,128)(2,1)}, bf16[96,2304]{1,0:T(8,128)(2,1)}, bf16[96,768]{1,0:T(8,128)(2,1)}, f32[6,1...) custom-call(bf16[2,1024,768]{2,1,0:T(8,128)(2,1)} %x_hbm.1, bf16[2,1024,768]{2,1,0:T(8,128)(2,1)} %dy_hbm.1, ...), custom_call_target="tpu_custom_call" | custom-call | tf_op jit(solution)/shard_map/xca_block/pallas_call | solution.py:596
  76.7 7.4 %finish.1 = (bf16[2,1024,768]{2,1,0:T(8,128)(2,1)}, bf16[2,1024,768]{2,1,0:T(8,128)(2,1)}, bf16[96,2304]{1,0:T(8,128)(2,1)}, bf16[96,768]{1,0:T(8,128)(2,1)}, f3...) custom-call(bf16[2048,768]{1,0:T(8,128)(2,1)} %get-tuple-element.14.y_hbm, bf16[2048,768]{1,0:T(8,128)(2,1)} %get-tuple-element.15.dx_hbm, ...), custom_call_target="tpu_custom_call" | custom-call | tf_op jit(solution)/shard_map/finish/pallas_call | solution.py:651

commit v3 on v2

--- a/solution.py
+++ b/solution.py
@@ -27,7 +27,7 @@
     x_hbm, dy_hbm, gain_hbm, bias_hbm, wqkv_hbm, wo_hbm, tau_hbm,
     y_hbm, dx_hbm, dwqkv_ref, dwo_ref, dgain_ref, dbias_ref, dtau_ref,
     gain_ref, bias_ref, tau_ref, x_v, dy_v, w_v, wt_v, wo_v, ut, zt, dot_v, ot,
-    sq_acc, gs_out, gs_in, gs_sum, a_all, ds_out, ds_in, g_all, c_all, bd, colq, colk, dgb, gb_all,
+    sq_acc, gs_out, gs_mid, gs_in, gs_sum, a_all, ds_out, ds_mid, ds_in, g_all, c_all, bd, colq, colk, dgb, gb_all,
     part, r1, r2, r3,
     in_sem, out_sem, d2d_s, d2d_r, p1_s, p1_r, p2_s, p2_r,
     gs_s, gs_r, a_s, a_r, ds_s, ds_r, g_s, g_r, c_s, c_r, gb_s, gb_r,
@@ -68,14 +68,15 @@
     cp_small = [pltpu.make_async_copy(h, v, in_sem.at[base + i]) for i, (h, v) in enumerate(
         ((gain_hbm, gain_ref), (bias_hbm, bias_ref), (tau_hbm, tau_ref)))]
     base += 3
-    cp_wqk = pltpu.make_async_copy(wqkv_hbm.at[:, pl.ds(0, 2 * dim)], w_v.at[:, pl.ds(0, 2 * dim)], in_sem.at[base])
-    cp_wv = pltpu.make_async_copy(wqkv_hbm.at[:, pl.ds(2 * dim, dim)], w_v.at[:, pl.ds(2 * dim, dim)], in_sem.at[base + 1])
-    cp_wo = pltpu.make_async_copy(wo_hbm, wo_v, in_sem.at[base + 2])
+    cp_wq, cp_wk, cp_wv = [pltpu.make_async_copy(wqkv_hbm.at[:, pl.ds(i * dim, dim)], w_v.at[:, pl.ds(i * dim, dim)], in_sem.at[base + i])
+                           for i in range(3)]
+    cp_wo = pltpu.make_async_copy(wo_hbm, wo_v, in_sem.at[base + 3])
     for c in cp_small:
         c.start()
     cp_x(0, 0).start()
-    cp_wqk.start()
+    cp_wq.start()
     cp_x(0, 1).start()
+    cp_wk.start()
 
     barrier = pltpu.get_barrier_semaphore()
     for k in peers:
@@ -107,6 +108,27 @@
             wt_v[pl.ds(off, COLS), :] = w_v[:, pl.ds(off, COLS)].T
             return 0
         lax.fori_loop(0, count // COLS, body, 0)
+
+    other_chips = range(1, chips)
+
+    def pair_sum(out, mid, ss, rs, b):
+        return rcopy(out.at[b, 1 - core], mid.at[b], ss.at[b, 0], rs.at[b, 0], partner)
+
+    def chip_copy(out, into, ss, rs, b, k):
+        to = (chip + k) % chips
+        return rcopy(out.at[b, core, to], into.at[b, k], ss.at[b, k], rs.at[b, k], to * 2 + core)
+
+    def scatter_state(out, mid, into, ss, rs, b):
+        pair_sum(out, mid, ss, rs, b).wait_recv()
+        out[b, core] += mid[b]
+        for k in (2, 1, 3):
+            chip_copy(out, into, ss, rs, b, k).start()
+
+    def state_total(out, into, ss, rs, b):
+        tot = out[b, core, chip]
+        for k in other_chips:
+            tot = tot + into[b, k]
+        return tot
 
     lane_w = lax.broadcasted_iota(jnp.int32, (hd, LANES), 1)
 
@@ -126,7 +148,7 @@
                     for s in range(2):
                         r0 = (2 * d + s) * hd
                         rest = jnp.where(lane_w == 2 * hd + 2 * i + s, col[r0:r0 + hd], rest)
-            out_ref[d] = jnp.where(lane_w < hd, picked[0], jnp.where(lane_w < 2 * hd, picked[1], rest))
+            out_ref[d % 2, d // 2] = jnp.where(lane_w < hd, picked[0], jnp.where(lane_w < 2 * hd, picked[1], rest))
 
     def gram(b, l_ref, l0, r_ref, r0):
         blocks = []
@@ -143,6 +165,8 @@
         return blocks
 
     def qk_tile(off, following, wt_cols=None):
+        if wt_cols == dim:
+            wt_v[dim:2 * dim, :] = w_v[:, dim:2 * dim].T
         for m in range(2):
             z = mm(wt_v[m * dim:(m + 1) * dim, :], ut[:, pl.ds(off, TOK)]).astype(BF16)
             zt[m * dim:(m + 1) * dim, pl.ds(off, TOK)] = z
@@ -154,7 +178,7 @@
             sq_acc[off // tokens, m * dim:(m + 1) * dim] += tot
         if following is not None:
             norm_rows(following, TOK)
-        if wt_cols is not None:
+        if wt_cols is not None and wt_cols > dim:
             wt_v[wt_cols:wt_cols + dim // 2, :] = w_v[:, wt_cols:wt_cols + dim // 2].T
 
     def send_gram(b):
@@ -162,33 +186,30 @@
         to_pairs(gram(b, zt, 0, zt, dim), gs_out.at[b], cols)
         if b == 0:
             pl.semaphore_wait(barrier, n - 1)
-        for k in far_first:
-            dst = (me + k) % n
-            rcopy(gs_out.at[b, dst], gs_in.at[b, k], gs_s.at[b, k], gs_r.at[b, k], dst).start()
+        pair_sum(gs_out, gs_mid, gs_s, gs_r, b).start()
 
     for b in range(1, images):
         for t in range(tiles):
             cp_x(b, t).start()
     norm_rows(0, TOK)
-    cp_x(0, 1).wait()
-    cp_wqk.wait()
+    cp_wq.wait()
     cp_wv.start()
     cp_wo.start()
     for b in range(images):
         cp_dy(b).start()
-    transpose_w(0, 2 * dim)
-
-    def qk_first(t, _):
-        off = pl.multiple_of(t * TOK, TOK)
-        qk_tile(off, off + TOK)
-        return 0
-    for b in range(1, images):
-        for t in range(tiles):
-            cp_x(b, t).wait()
-    lax.fori_loop(0, tiles, qk_first, 0)
+    transpose_w(0, dim)
+    cp_x(0, 1).wait()
+    cp_wk.wait()
+    qk_tile(0, TOK, dim)
+    for t in range(tiles):
+        cp_x(1, t).wait()
+    for t in range(1, tiles):
+        qk_tile(t * TOK, (t + 1) * TOK)
     send_gram(0)
     cp_wv.wait()
     for t in range(tiles):
+        if t == 1:
+            scatter_state(gs_out, gs_mid, gs_in, gs_s, gs_r, 0)
         off = tokens + t * TOK
         qk_tile(off, off + TOK if t + 1 < tiles else None, 2 * dim + t * dim // tiles)
     send_gram(1)
@@ -225,12 +246,9 @@
         return jnp.concatenate([a0, a1, z], axis=1)
 
     def owner_forward(b):
-        for k in peers:
-            rcopy(gs_out.at[b, 0], gs_in.at[b, k], gs_s.at[b, k], gs_r.at[b, k], me).wait_recv()
-        tot = gs_out[b, me]
-        for k in peers:
-            tot = tot + gs_in[b, k]
-        gs_sum[b] = tot
+        for k in other_chips:
+            chip_copy(gs_out, gs_in, gs_s, gs_r, b, k).wait_recv()
+        gs_sum[b] = state_total(gs_out, gs_in, gs_s, gs_r, b)
         p0 = attn_state(b, 0)[2]
         p1 = attn_state(b, 1)[2]
         a_all[b, me] = pair(p0, p1).astype(BF16)
@@ -240,15 +258,12 @@
 
     def owner_backward():
         for b in range(images):
-            for k in peers:
-                rcopy(ds_out.at[b, 0], ds_in.at[b, k], ds_s.at[b, k], ds_r.at[b, k], me).wait_recv()
+            for k in other_chips:
+                chip_copy(ds_out, ds_in, ds_s, ds_r, b, k).wait_recv()
         sub = lax.broadcasted_iota(jnp.int32, (8, LANES), 0)
         lane = lax.broadcasted_iota(jnp.int32, (8, LANES), 1)
         for b in range(images):
-            tot = ds_out[b, me]
-            for k in peers:
-                tot = tot + ds_in[b, k]
-            tot = tot.astype(BF16).astype(F32)
+            tot = state_total(ds_out, ds_in, ds_s, ds_r, b).astype(BF16).astype(F32)
             gs, qs, ks, ts = [], [], [], []
             for s in range(2):
                 cosine, logits, probs, scale, qc, kr = attn_state(b, s)
@@ -263,10 +278,26 @@
             taus = jnp.where(lane == 0, ts[0], jnp.where(lane == 1, ts[1], 0.0))
             c_all[b, me] = jnp.where(sub == 0, pair(qs[0], qs[1]), jnp.where(sub == 1, pair(ks[0], ks[1]), jnp.where(sub == 2, taus, 0.0)))
         for b in range(images):
-            for k in far_first:
-                dst = (me + k) % n
-                rcopy(g_all.at[b, me], g_all.at[b, me], g_s.at[b, k], g_r.at[b, k], dst).start()
-                rcopy(c_all.at[b, me], c_all.at[b, me], c_s.at[b, k], c_r.at[b, k], dst).start()
+            for ref, ss, rs in states:
+                for k in (4, 2, 6, 1):
+                    dst = (me + k) % n if k > 1 else partner
+                    rcopy(ref.at[b, me], ref.at[b, me], ss.at[b, k], rs.at[b, k], dst).start()
+
+    states = ((g_all, g_s, g_r), (c_all, c_s, c_r))
+
+    def pass_on(b):
+        for ref, ss, rs in states:
+            for k in (2, 6, 4):
+                src = (me + n - k) % n
+                rcopy(ref.at[b, me], ref.at[b, src], ss.at[b, k], rs.at[b, k], me).wait_recv()
+                rcopy(ref.at[b, src], ref.at[b, src], ss.at[b, k + 1], rs.at[b, k + 1], partner).start()
+
+    def passed(b):
+        for ref, ss, rs in states:
+            rcopy(ref.at[b, me], ref.at[b, partner], ss.at[b, 1], rs.at[b, 1], me).wait_recv()
+            for k in (2, 6, 4):
+                src = (partner + n - k) % n
+                rcopy(ref.at[b, me], ref.at[b, src], ss.at[b, k + 1], rs.at[b, k + 1], me).wait_recv()
 
     def gathered(ref, ss, rs, b):
         for k in peers:
@@ -284,9 +315,7 @@
 
     def send_dprobs(b):
         to_pairs(gram(b, dot_v, 0, zt, 2 * dim), ds_out.at[b])
-        for k in far_first:
-            dst = (me + k) % n
-            rcopy(ds_out.at[b, dst], ds_in.at[b, k], ds_s.at[b, k], ds_r.at[b, k], dst).start()
+        pair_sum(ds_out, ds_mid, ds_s, ds_r, b).start()
 
     sj = lax.broadcasted_iota(jnp.int32, (LANES, COLS), 0)
     slane = lax.broadcasted_iota(jnp.int32, (LANES, COLS), 1)
@@ -349,12 +378,9 @@
             return 0
         lax.fori_loop(0, tiles, body, 0)
 
-    def put_part(c, val, more=False):
+    def put_part(c, val):
         for j in range(n):
-            rows_j = val[j * per_dev:(j + 1) * per_dev, :]
-            if more:
-                rows_j += part[c, j % 2, j // 2]
-            part[c, j % 2, j // 2] = rows_j
+            part[c, j % 2, j // 2] = val[j * per_dev:(j + 1) * per_dev, :]
 
     def d2d(c):
         return rcopy(part.at[c, 1 - core], r1.at[c], d2d_s.at[c], d2d_r.at[c], partner)
@@ -389,12 +415,10 @@
             h.wait_recv()
         return (r1[c, chip] + r3[c, 0] + r3[c, 1]).astype(BF16)
 
-    def wo_chunk(c, b):
+    def wo_chunk(c):
         off = pl.multiple_of(c * COLS, COLS)
-        tok_b = slice(b * tokens, (b + 1) * tokens)
-        put_part(c, mm(ot[:, tok_b], dy_v[tok_b, pl.ds(off, COLS)]), b > 0)
-        if b + 1 == images:
-            d2d(c).start()
+        put_part(c, mm(ot[...], dy_v[:, pl.ds(off, COLS)]))
+        d2d(c).start()
 
     def qkv_chunk(c, base):
         off = pl.multiple_of(base + c * COLS, COLS)
@@ -402,22 +426,31 @@
         d2d(c).start()
 
     values(0)
+    scatter_state(gs_out, gs_mid, gs_in, gs_s, gs_r, 1)
     grad_heads(0)
     owner_forward(0)
     send_dprobs(0)
     values(1)
+    scatter_state(ds_out, ds_mid, ds_in, ds_s, ds_r, 0)
     owner_forward(1)
     grad_heads(1)
     send_dprobs(1)
-    for b in range(images):
-        gathered(a_all, a_s, a_r, b)
-        build(a_all, b)
-        heads_out(b)
-
-        for c in range(o_chunks):
-            wo_chunk(c, b)
-            if b + 1 == images and c > 0:
-                serve1(c - 1)
+    gathered(a_all, a_s, a_r, 0)
+    build(a_all, 0)
+    heads_out(0)
+    scatter_state(ds_out, ds_mid, ds_in, ds_s, ds_r, 1)
+    gathered(a_all, a_s, a_r, 1)
+    build(a_all, 1)
+    heads_out(1)
+
+    def wo_loop(c, _):
+        wo_chunk(c)
+
+        @pl.when(c > 0)
+        def _():
+            serve1(c - 1)
+        return 0
+    lax.fori_loop(0, o_chunks, wo_loop, 0)
     owner_backward()
     serve1(o_chunks - 1)
     grad_values(0)
@@ -439,10 +472,11 @@
         serve1(c - 1)
         return 0
     lax.fori_loop(o_chunks + 1, 2 * o_chunks, v_loop, 0)
+    for b in range(images):
+        pass_on(b)
     serve2_range(2, 3)
     for b in range(images):
-        gathered(g_all, g_s, g_r, b)
-        gathered(c_all, c_s, c_r, b)
+        passed(b)
         build(g_all, b)
         dq_and_dk(b)
         if b == 0:
@@ -470,7 +504,9 @@
         def piece(i, _):
             r = pl.ds(pl.multiple_of(off + i * LANES, LANES), LANES)
             du = dot_v[:, r].T.astype(F32)
-            x_hat, inv = norm(x_v[r, :].astype(F32))
+            xt = x_v[r, :].astype(F32)
+            x_v[r, :] = (xt + mm(ot[:, r].T, wo_v[...])).astype(BF16)
+            x_hat, inv = norm(xt)
             prod = du * x_hat
             dgb[0] += jnp.sum(prod.reshape(LANES // 8, 8, dim), axis=0)
             dgb[1] += jnp.sum(du.reshape(LANES // 8, 8, dim), axis=0)
@@ -481,21 +517,16 @@
             dy_v[r, :] = (dy_v[r, :].astype(F32) + gx).astype(BF16)
             return 0
         lax.fori_loop(0, TOK // LANES, piece, 0)
+        tile_copy(0, t).start()
         tile_copy(1, t).start()
         return 0
 
-    def y_body(t, _):
-        off = pl.multiple_of(t * TOK, TOK)
-        x_v[pl.ds(off, TOK), :] = (x_v[pl.ds(off, TOK), :].astype(F32) + mm(ot[:, pl.ds(off, TOK)].T, wo_v[...])).astype(BF16)
-        tile_copy(0, t).start()
-        return 0
     lax.fori_loop(0, 1, dx_body, 0)
     serve2_range(chunks - 3, chunks)
     lax.fori_loop(1, images * tiles, dx_body, 0)
     gb_all[me] = jnp.concatenate([jnp.sum(dgb[i], axis=0).reshape(dim // LANES, LANES) for i in range(2)], axis=0)
     for k in far_first:
         rcopy(gb_all.at[me], gb_all.at[me], gb_s.at[k], gb_r.at[k], (me + k) % n).start()
-    lax.fori_loop(0, images * tiles, y_body, 0)
 
     lane = lax.broadcasted_iota(jnp.int32, (1, LANES), 1)
     dtau = jnp.zeros((1, LANES), F32)
@@ -533,10 +564,12 @@
     lax.fori_loop(2 * o_chunks, chunks, s3_qk, 0)
 
     for b in range(images):
+        for out, mid, into, ss, rs in ((gs_out, gs_mid, gs_in, gs_s, gs_r), (ds_out, ds_mid, ds_in, ds_s, ds_r)):
+            pair_sum(out, mid, ss, rs, b).wait_send()
+            for k in other_chips:
+                chip_copy(out, into, ss, rs, b, k).wait_send()
         for k in peers:
-            rcopy(gs_out.at[b, 0], gs_in.at[b, k], gs_s.at[b, k], gs_r.at[b, k], me).wait_send()
             rcopy(a_all.at[b, me], a_all.at[b, me], a_s.at[b, k], a_r.at[b, k], me).wait_send()
-            rcopy(ds_out.at[b, 0], ds_in.at[b, k], ds_s.at[b, k], ds_r.at[b, k], me).wait_send()
             rcopy(g_all.at[b, me], g_all.at[b, me], g_s.at[b, k], g_r.at[b, k], me).wait_send()
             rcopy(c_all.at[b, me], c_all.at[b, me], c_s.at[b, k], c_r.at[b, k], me).wait_send()
     for k in peers:
@@ -620,12 +653,14 @@
                 pltpu.VMEM((dim, rows), BF16),
                 pltpu.VMEM((dim, rows), BF16),
                 pltpu.VMEM((images, 2 * dim, LANES), F32),
-                pltpu.VMEM((images, n, hd, LANES), F32),
-                pltpu.VMEM((images, n, hd, LANES), F32),
+                pltpu.VMEM((images, 2, n // 2, hd, LANES), F32),
+                pltpu.VMEM((images, n // 2, hd, LANES), F32),
+                pltpu.VMEM((images, n // 2, hd, LANES), F32),
                 pltpu.VMEM((images, hd, LANES), F32),
                 pltpu.VMEM((images, n, hd, LANES), BF16),
-                pltpu.VMEM((images, n, hd, LANES), F32),
-                pltpu.VMEM((images, n, hd, LANES), F32),
+                pltpu.VMEM((images, 2, n // 2, hd, LANES), F32),
+                pltpu.VMEM((images, n // 2, hd, LANES), F32),
+                pltpu.VMEM((images, n // 2, hd, LANES), F32),
                 pltpu.VMEM((images, n, hd, LANES), BF16),
                 pltpu.VMEM((images, n, 8, LANES), F32),
                 pltpu.VMEM((images, nwin, 2, COLS, COLS), BF16),
@@ -637,7 +672,7 @@
                 pltpu.VMEM((chunks, n // 2, per_dev, COLS), F32),
                 pltpu.VMEM((chunks, 2, per_dev // 2, COLS), F32),
                 pltpu.VMEM((chunks, 2, per_dev, COLS), F32),
-                dma((rows // TOK + images + 6,)), dma((2, rows // TOK)),
+                dma((rows // TOK + images + 7,)), dma((2, rows // TOK)),
                 dma((chunks,)), dma((chunks,)),
                 dma((chunks, 2)), dma((chunks, 2)), dma((chunks, 2)), dma((chunks, 2)),
                 dma(pairs), dma(pairs), dma(pairs), dma(pairs), dma(pairs), dma(pairs),

time: 84.4 us -> 82.1 us (0.973)
  Pallas kernels: 83.5 us -> 81.2 us
    pallas_call x1, Pallas kernels: 76.1 us -> 73.8 us  [local_step(): pl.pallas_call(functools.partial(xca_kernel, n, heads), out_shape=(jax.Sh...]
where the time goes in v3:
time: 82.1 us; the launch traced here: 82 us
  Pallas kernels  81.2 us (99%)
    pallas_call x1, Pallas kernels, local_step(): pl.pallas_call(functools.partial(xca_kernel, n, heads), out_shape=(jax.Sh...  73.8 us
    pallas_call x1, Pallas kernels, local_step(): pl.pallas_call(functools.partial(finish_kernel, heads), out_shape=(jax.Sh...  7.44 us

profile of v3, /device:TPU:113, one launch (start us, length us, event | category | flops | bytes accessed | tf_op | source)
XLA Modules:
  0.0 82.0 jit_solution(8961372025693889892)
XLA Ops:
  0.6 73.8 %xca_block.1 = (bf16[2048,768]{1,0:T(8,128)(2,1)}, bf16[2048,768]{1,0:T(8,128)(2,1)}, bf16[96,2304]{1,0:T(8,128)(2,1)}, bf16[96,768]{1,0:T(8,128)(2,1)}, f32[6,1...) custom-call(bf16[2,1024,768]{2,1,0:T(8,128)(2,1)} %x_hbm.1, bf16[2,1024,768]{2,1,0:T(8,128)(2,1)} %dy_hbm.1, ...), custom_call_target="tpu_custom_call" | custom-call | tf_op jit(solution)/shard_map/xca_block/pallas_call | solution.py:629
  74.4 7.4 %finish.1 = (bf16[2,1024,768]{2,1,0:T(8,128)(2,1)}, bf16[2,1024,768]{2,1,0:T(8,128)(2,1)}, bf16[96,2304]{1,0:T(8,128)(2,1)}, bf16[96,768]{1,0:T(8,128)(2,1)}, f3...) custom-call(bf16[2048,768]{1,0:T(8,128)(2,1)} %get-tuple-element.14.y_hbm, bf16[2048,768]{1,0:T(8,128)(2,1)} %get-tuple-element.15.dx_hbm, ...), custom_call_target="tpu_custom_call" | custom-call | tf_op jit(solution)/shard_map/finish/pallas_call | solution.py:686

commit v4 on v3

--- a/solution.py
+++ b/solution.py
@@ -25,11 +25,11 @@
 def xca_kernel(
     n, heads,
     x_hbm, dy_hbm, gain_hbm, bias_hbm, wqkv_hbm, wo_hbm, tau_hbm,
-    y_hbm, dx_hbm, dwqkv_ref, dwo_ref, dgain_ref, dbias_ref, dtau_ref,
-    gain_ref, bias_ref, tau_ref, x_v, dy_v, w_v, wt_v, wo_v, ut, zt, dot_v, ot,
+    y_hbm, dx_hbm, dwqkv_hbm, dwo_hbm, dgain_hbm, dbias_hbm, dtau_hbm,
+    dwqkv_ref, dwo_ref, dgain_ref, dbias_ref, dtau_ref, gain_ref, bias_ref, tau_ref, x_v, dy_v, w_v, wt_v, wo_v, ut, zt, dot_v, ot,
     sq_acc, gs_out, gs_mid, gs_in, gs_sum, a_all, ds_out, ds_mid, ds_in, g_all, c_all, bd, colq, colk, dgb, gb_all,
     part, r1, r2, r3,
-    in_sem, out_sem, d2d_s, d2d_r, p1_s, p1_r, p2_s, p2_r,
+    in_sem, out_sem, w_sem, d2d_s, d2d_r, p1_s, p1_r, p2_s, p2_r,
     gs_s, gs_r, a_s, a_r, ds_s, ds_r, g_s, g_r, c_s, c_r, gb_s, gb_r,
 ):
     images, tokens, dim = x_hbm.shape
@@ -89,6 +89,9 @@
         c.wait()
     cp_x(0, 0).wait()
 
+    def phase(f, *args):
+        f(*args)
+
     def norm(xt):
         mean = jnp.sum(xt, axis=-1, keepdims=True) * (1.0 / dim)
         cen = xt - mean
@@ -112,11 +115,11 @@
     other_chips = range(1, chips)
 
     def pair_sum(out, mid, ss, rs, b):
-        return rcopy(out.at[b, 1 - core], mid.at[b], ss.at[b, 0], rs.at[b, 0], partner)
+        return rcopy(out.at[b, 1 - core], mid.at[b], ss.at[0], rs.at[b, 0], partner)
 
     def chip_copy(out, into, ss, rs, b, k):
         to = (chip + k) % chips
-        return rcopy(out.at[b, core, to], into.at[b, k], ss.at[b, k], rs.at[b, k], to * 2 + core)
+        return rcopy(out.at[b, core, to], into.at[b, k], ss.at[1], rs.at[b, k], to * 2 + core)
 
     def scatter_state(out, mid, into, ss, rs, b):
         pair_sum(out, mid, ss, rs, b).wait_recv()
@@ -191,7 +194,7 @@
     for b in range(1, images):
         for t in range(tiles):
             cp_x(b, t).start()
-    norm_rows(0, TOK)
+    phase(norm_rows, 0, TOK)
     cp_wq.wait()
     cp_wv.start()
     cp_wo.start()
@@ -200,19 +203,19 @@
     transpose_w(0, dim)
     cp_x(0, 1).wait()
     cp_wk.wait()
-    qk_tile(0, TOK, dim)
+    phase(qk_tile, 0, TOK, dim)
     for t in range(tiles):
         cp_x(1, t).wait()
     for t in range(1, tiles):
-        qk_tile(t * TOK, (t + 1) * TOK)
-    send_gram(0)
+        phase(qk_tile, t * TOK, (t + 1) * TOK)
+    phase(send_gram, 0)
     cp_wv.wait()
     for t in range(tiles):
         if t == 1:
-            scatter_state(gs_out, gs_mid, gs_in, gs_s, gs_r, 0)
+            phase(scatter_state, gs_out, gs_mid, gs_in, gs_s, gs_r, 0)
         off = tokens + t * TOK
-        qk_tile(off, off + TOK if t + 1 < tiles else None, 2 * dim + t * dim // tiles)
-    send_gram(1)
+        phase(qk_tile, off, off + TOK if t + 1 < tiles else None, 2 * dim + t * dim // tiles)
+    phase(send_gram, 1)
 
     def values(b):
         for t in range(tiles):
@@ -254,7 +257,7 @@
         a_all[b, me] = pair(p0, p1).astype(BF16)
         for k in far_first:
             dst = (me + k) % n
-            rcopy(a_all.at[b, me], a_all.at[b, me], a_s.at[b, k], a_r.at[b, k], dst).start()
+            rcopy(a_all.at[b, me], a_all.at[b, me], a_s.at[0], a_r.at[b, k], dst).start()
 
     def owner_backward():
         for b in range(images):
@@ -281,7 +284,7 @@
             for ref, ss, rs in states:
                 for k in (4, 2, 6, 1):
                     dst = (me + k) % n if k > 1 else partner
-                    rcopy(ref.at[b, me], ref.at[b, me], ss.at[b, k], rs.at[b, k], dst).start()
+                    rcopy(ref.at[b, me], ref.at[b, me], ss.at[0], rs.at[b, k], dst).start()
 
     states = ((g_all, g_s, g_r), (c_all, c_s, c_r))
 
@@ -289,20 +292,20 @@
         for ref, ss, rs in states:
             for k in (2, 6, 4):
                 src = (me + n - k) % n
-                rcopy(ref.at[b, me], ref.at[b, src], ss.at[b, k], rs.at[b, k], me).wait_recv()
-                rcopy(ref.at[b, src], ref.at[b, src], ss.at[b, k + 1], rs.at[b, k + 1], partner).start()
+                rcopy(ref.at[b, me], ref.at[b, src], ss.at[0], rs.at[b, k], me).wait_recv()
+                rcopy(ref.at[b, src], ref.at[b, src], ss.at[0], rs.at[b, k + 1], partner).start()
 
     def passed(b):
         for ref, ss, rs in states:
-            rcopy(ref.at[b, me], ref.at[b, partner], ss.at[b, 1], rs.at[b, 1], me).wait_recv()
+            rcopy(ref.at[b, me], ref.at[b, partner], ss.at[0], rs.at[b, 1], me).wait_recv()
             for k in (2, 6, 4):
                 src = (partner + n - k) % n
-                rcopy(ref.at[b, me], ref.at[b, src], ss.at[b, k + 1], rs.at[b, k + 1], me).wait_recv()
+                rcopy(ref.at[b, me], ref.at[b, src], ss.at[0], rs.at[b, k + 1], me).wait_recv()
 
     def gathered(ref, ss, rs, b):
         for k in peers:
             src = (me + n - k) % n
-            rcopy(ref.at[b, me], ref.at[b, src], ss.at[b, k], rs.at[b, k], me).wait_recv()
+            rcopy(ref.at[b, me], ref.at[b, src], ss.at[0], rs.at[b, k], me).wait_recv()
 
     def grad_heads(b):
         cp_dy(b).wait()
@@ -383,17 +386,17 @@
             part[c, j % 2, j // 2] = val[j * per_dev:(j + 1) * per_dev, :]
 
     def d2d(c):
-        return rcopy(part.at[c, 1 - core], r1.at[c], d2d_s.at[c], d2d_r.at[c], partner)
+        return rcopy(part.at[c, 1 - core], r1.at[c], d2d_s.at[0], d2d_r.at[c], partner)
 
     half = per_dev // 2
 
     def hop1(c):
-        return (rcopy(r1.at[c, co, pl.ds(0, half)], r2.at[c, 0], p1_s.at[c, 0], p1_r.at[c, 0], right),
-                rcopy(r1.at[c, co, pl.ds(half, half)], r2.at[c, 1], p1_s.at[c, 1], p1_r.at[c, 1], left))
+        return (rcopy(r1.at[c, co, pl.ds(0, half)], r2.at[c, 0], p1_s.at[0], p1_r.at[c, 0], right),
+                rcopy(r1.at[c, co, pl.ds(half, half)], r2.at[c, 1], p1_s.at[0], p1_r.at[c, 1], left))
 
     def hop2(c):
-        return (rcopy(r1.at[c, cr], r3.at[c, 0], p2_s.at[c, 0], p2_r.at[c, 0], right),
-                rcopy(r1.at[c, cl], r3.at[c, 1], p2_s.at[c, 1], p2_r.at[c, 1], left))
+        return (rcopy(r1.at[c, cr], r3.at[c, 0], p2_s.at[0], p2_r.at[c, 0], right),
+                rcopy(r1.at[c, cl], r3.at[c, 1], p2_s.at[0], p2_r.at[c, 1], left))
 
     def serve1(c):
         d2d(c).wait_recv()
@@ -425,23 +428,23 @@
         put_part(c, mm(ut[...], zt[pl.ds(off, COLS), :], NT))
         d2d(c).start()
 
-    values(0)
-    scatter_state(gs_out, gs_mid, gs_in, gs_s, gs_r, 1)
-    grad_heads(0)
-    owner_forward(0)
-    send_dprobs(0)
-    values(1)
-    scatter_state(ds_out, ds_mid, ds_in, ds_s, ds_r, 0)
-    owner_forward(1)
-    grad_heads(1)
-    send_dprobs(1)
+    phase(values, 0)
+    phase(scatter_state, gs_out, gs_mid, gs_in, gs_s, gs_r, 1)
+    phase(grad_heads, 0)
+    phase(owner_forward, 0)
+    phase(send_dprobs, 0)
+    phase(values, 1)
+    phase(scatter_state, ds_out, ds_mid, ds_in, ds_s, ds_r, 0)
+    phase(owner_forward, 1)
+    phase(grad_heads, 1)
+    phase(send_dprobs, 1)
     gathered(a_all, a_s, a_r, 0)
-    build(a_all, 0)
-    heads_out(0)
-    scatter_state(ds_out, ds_mid, ds_in, ds_s, ds_r, 1)
+    phase(build, a_all, 0)
+    phase(heads_out, 0)
+    phase(scatter_state, ds_out, ds_mid, ds_in, ds_s, ds_r, 1)
     gathered(a_all, a_s, a_r, 1)
-    build(a_all, 1)
-    heads_out(1)
+    phase(build, a_all, 1)
+    phase(heads_out, 1)
 
     def wo_loop(c, _):
         wo_chunk(c)
@@ -451,7 +454,7 @@
             serve1(c - 1)
         return 0
     lax.fori_loop(0, o_chunks, wo_loop, 0)
-    owner_backward()
+    phase(owner_backward)
     serve1(o_chunks - 1)
     grad_values(0)
     grad_values(1)
@@ -477,7 +480,7 @@
     serve2_range(2, 3)
     for b in range(images):
         passed(b)
-        build(g_all, b)
+        phase(build, g_all, b)
         dq_and_dk(b)
         if b == 0:
             serve1(2 * o_chunks - 1)
@@ -495,7 +498,7 @@
     def tile_copy(i, t):
         rows_t = pl.ds(pl.multiple_of(t * TOK, TOK), TOK)
         src, dst = ((x_v, y_hbm), (dy_v, dx_hbm))[i]
-        return pltpu.make_async_copy(src.at[rows_t], dst.at[rows_t], out_sem.at[i, t])
+        return pltpu.make_async_copy(src.at[rows_t], dst.at[rows_t], out_sem.at[i])
 
     def dx_body(t, _):
         off = pl.multiple_of(t * TOK, TOK)
@@ -526,7 +529,7 @@
     lax.fori_loop(1, images * tiles, dx_body, 0)
     gb_all[me] = jnp.concatenate([jnp.sum(dgb[i], axis=0).reshape(dim // LANES, LANES) for i in range(2)], axis=0)
     for k in far_first:
-        rcopy(gb_all.at[me], gb_all.at[me], gb_s.at[k], gb_r.at[k], (me + k) % n).start()
+        rcopy(gb_all.at[me], gb_all.at[me], gb_s.at[0], gb_r.at[k], (me + k) % n).start()
 
     lane = lax.broadcasted_iota(jnp.int32, (1, LANES), 1)
     dtau = jnp.zeros((1, LANES), F32)
@@ -539,72 +542,78 @@
         dtau = jnp.where(jnp.logical_and(lane >= 2 * d, lane < 2 * d + 2), row, dtau)
     dtau_ref[...] = dtau
 
-    def s3_wo(c, _):
-        dwo_ref[:, pl.ds(pl.multiple_of(c * COLS, COLS), COLS)] = serve3(c)
-        return 0
-    lax.fori_loop(0, o_chunks, s3_wo, 0)
-
-    def s3_v(c, _):
-        dwqkv_ref[:, pl.ds(pl.multiple_of(2 * dim - dim + c * COLS, COLS), COLS)] = serve3(c)
-        return 0
-    lax.fori_loop(o_chunks, 2 * o_chunks, s3_v, 0)
+    def chunk_copy(c, src, dst, base, which):
+        cols = pl.ds(pl.multiple_of(base + c * COLS, COLS), COLS)
+        return pltpu.make_async_copy(src.at[:, cols], dst.at[:, cols], w_sem.at[which])
+
+    def finish_chunks(c0, c1, src, dst, base, which):
+        def body(c, _):
+            src[:, pl.ds(pl.multiple_of(base + c * COLS, COLS), COLS)] = serve3(c)
+            chunk_copy(c, src, dst, base, which).start()
+            return 0
+        lax.fori_loop(c0, c1, body, 0)
+
+    finish_chunks(0, o_chunks, dwo_ref, dwo_hbm, 0, 0)
+    finish_chunks(o_chunks, 2 * o_chunks, dwqkv_ref, dwqkv_hbm, v0, 1)
 
     for k in peers:
         src = (me + n - k) % n
-        rcopy(gb_all.at[me], gb_all.at[src], gb_s.at[k], gb_r.at[k], me).wait_recv()
+        rcopy(gb_all.at[me], gb_all.at[src], gb_s.at[0], gb_r.at[k], me).wait_recv()
     tot = gb_all[0]
-    for d in range(1, n):
+    for d in peers:
         tot = tot + gb_all[d]
     dgain_ref[...] = tot[:dim // LANES]
     dbias_ref[...] = tot[dim // LANES:]
-
-    def s3_qk(c, _):
-        dwqkv_ref[:, pl.ds(pl.multiple_of(c * COLS - 2 * dim, COLS), COLS)] = serve3(c)
-        return 0
-    lax.fori_loop(2 * o_chunks, chunks, s3_qk, 0)
-
-    for b in range(images):
-        for out, mid, into, ss, rs in ((gs_out, gs_mid, gs_in, gs_s, gs_r), (ds_out, ds_mid, ds_in, ds_s, ds_r)):
-            pair_sum(out, mid, ss, rs, b).wait_send()
-            for k in other_chips:
-                chip_copy(out, into, ss, rs, b, k).wait_send()
-        for k in peers:
-            rcopy(a_all.at[b, me], a_all.at[b, me], a_s.at[b, k], a_r.at[b, k], me).wait_send()
-            rcopy(g_all.at[b, me], g_all.at[b, me], g_s.at[b, k], g_r.at[b, k], me).wait_send()
-            rcopy(c_all.at[b, me], c_all.at[b, me], c_s.at[b, k], c_r.at[b, k], me).wait_send()
-    for k in peers:
-        rcopy(gb_all.at[me], gb_all.at[me], gb_s.at[k], gb_r.at[k], me).wait_send()
-
-    def drain(c, _):
-        d2d(c).wait_send()
-        for h in hop1(c) + hop2(c):
-            h.wait_send()
-        return 0
-    lax.fori_loop(0, chunks, drain, 0)
-    for i in range(2):
-        for t in range(images * tiles):
-            tile_copy(i, t).wait()
-
-
-def finish_kernel(heads, y_hbm, dx_hbm, dwqkv_ref, dwo_ref, dgain_ref, dbias_ref, dtau_ref,
-                  y_out, dx_out, dwqkv_out, dwo_out, dgain_out, dbias_out, dtau_out, buf, sem_in, sem_out):
-    images, tokens, dim = y_out.shape
+    small_copies = [pltpu.make_async_copy(v, h, w_sem.at[2 + i]) for i, (v, h) in enumerate(
+        ((dgain_ref, dgain_hbm), (dbias_ref, dbias_hbm), (dtau_ref, dtau_hbm)))]
+    for c in small_copies:
+        c.start()
+    finish_chunks(2 * o_chunks, chunks, dwqkv_ref, dwqkv_hbm, -2 * o_chunks * COLS, 1)
+
+    sent = (
+        (gs_mid, gs_s, 0), (gs_in.at[:, pl.ds(1, chips - 1)], gs_s, 1),
+        (ds_mid, ds_s, 0), (ds_in.at[:, pl.ds(1, chips - 1)], ds_s, 1),
+        (a_all.at[:, pl.ds(0, n - 1)], a_s, 0), (g_all.at[:, pl.ds(0, n - 1)], g_s, 0), (c_all.at[:, pl.ds(0, n - 1)], c_s, 0),
+        (gb_all.at[pl.ds(0, n - 1)], gb_s, 0), (r1, d2d_s, 0), (r2, p1_s, 0), (r3, p2_s, 0))
+    for ref, sem, i in sent:
+        rcopy(ref, ref, sem.at[i], gb_r.at[0], partner).wait_send()
+    pltpu.make_async_copy(x_v, y_hbm, out_sem.at[0]).wait()
+    pltpu.make_async_copy(dy_v, dx_hbm, out_sem.at[1]).wait()
+    for c in small_copies:
+        c.wait()
+    pltpu.make_async_copy(dwo_ref, dwo_hbm, w_sem.at[0]).wait()
+    pltpu.make_async_copy(dwqkv_ref, dwqkv_hbm, w_sem.at[1]).wait()
+
+
+def finish_kernel(heads, y_hbm, dx_hbm, *refs):
+    moved, outputs, (buf, *stage, sem_in, sem_out) = refs[:5], refs[5:12], refs[12:]
+    landed, shaped = stage[:5], stage[:2] + stage[5:]
+    images, tokens, _dim = outputs[0].shape
     parts = tokens // TOK
     ins, outs = [], []
-    for src, dst in ((y_hbm, y_out), (dx_hbm, dx_out)):
+
+    def copy(src, dst, sem, into):
+        into.append(pltpu.make_async_copy(src, dst, sem.at[len(into)]))
+
+    for src, dst in ((y_hbm, outputs[0]), (dx_hbm, outputs[1])):
         for b in range(images):
             for t in range(parts):
-                i = len(ins)
-                ins.append(pltpu.make_async_copy(src.at[pl.ds((b * parts + t) * TOK, TOK)], buf.at[i], sem_in.at[i]))
-                outs.append(pltpu.make_async_copy(buf.at[i], dst.at[b, pl.ds(t * TOK, TOK)], sem_out.at[i]))
+                slot = buf.at[len(ins)]
+                copy(src.at[pl.ds((b * parts + t) * TOK, TOK)], slot, sem_in, ins)
+                copy(slot, dst.at[b, pl.ds(t * TOK, TOK)], sem_out, outs)
+    big = len(ins)
+    for src, mid, last, dst in zip(moved, landed, shaped, outputs[2:]):
+        copy(src, mid, sem_in, ins)
+        copy(last, dst, sem_out, outs)
     for c in ins:
         c.start()
-    dwqkv_out[...] = dwqkv_ref[...]
-    dwo_out[...] = dwo_ref[...]
-    dgain_out[...] = dgain_ref[...].reshape(dgain_out.shape)
-    dbias_out[...] = dbias_ref[...].reshape(dbias_out.shape)
-    dtau_out[...] = dtau_ref[...].reshape(dtau_ref.shape[1])[:heads]
-    for c, o in zip(ins, outs):
+    for c in ins[big:]:
+        c.wait()
+    for mid, last in zip(landed[2:], shaped[2:]):
+        last[...] = mid[...].reshape(mid.size)[:last.shape[0]]
+    for o in outs[big:]:
+        o.start()
+    for c, o in zip(ins[:big], outs[:big]):
         c.wait()
         o.start()
     for o in outs:
@@ -623,9 +632,9 @@
         chunks = 4 * dim // COLS
         nwin = -(-heads // (COLS // hd))
         any_spec = pl.BlockSpec(memory_space=pl.ANY)
-        vmem = pl.BlockSpec(memory_space=pltpu.VMEM)
         dma = pltpu.SemaphoreType.DMA
         pairs = (images, n)
+        one, by_chip = dma((1,)), dma((images, n // 2))
         out = pl.pallas_call(
             functools.partial(xca_kernel, n, heads),
             out_shape=(
@@ -638,8 +647,13 @@
                 jax.ShapeDtypeStruct((1, LANES), F32),
             ),
             in_specs=[any_spec] * 7,
-            out_specs=(any_spec,) * 2 + (vmem,) * 5,
+            out_specs=(any_spec,) * 7,
             scratch_shapes=[
+                pltpu.VMEM((per_dev, 3 * dim), BF16),
+                pltpu.VMEM((per_dev, dim), BF16),
+                pltpu.VMEM((dim // LANES, LANES), F32),
+                pltpu.VMEM((dim // LANES, LANES), F32),
+                pltpu.VMEM((1, LANES), F32),
                 pltpu.VMEM((dim,), F32),
                 pltpu.VMEM((dim,), F32),
                 pltpu.VMEM((heads,), F32),
@@ -672,12 +686,10 @@
                 pltpu.VMEM((chunks, n // 2, per_dev, COLS), F32),
                 pltpu.VMEM((chunks, 2, per_dev // 2, COLS), F32),
                 pltpu.VMEM((chunks, 2, per_dev, COLS), F32),
-                dma((rows // TOK + images + 7,)), dma((2, rows // TOK)),
-                dma((chunks,)), dma((chunks,)),
-                dma((chunks, 2)), dma((chunks, 2)), dma((chunks, 2)), dma((chunks, 2)),
-                dma(pairs), dma(pairs), dma(pairs), dma(pairs), dma(pairs), dma(pairs),
-                dma(pairs), dma(pairs), dma(pairs), dma(pairs),
-                dma((n,)), dma((n,)),
+                dma((rows // TOK + images + 7,)), dma((2,)), dma((5,)),
+                one, dma((chunks,)), one, dma((chunks, 2)), one, dma((chunks, 2)),
+                dma((2,)), by_chip, one, dma(pairs), dma((2,)), by_chip,
+                one, dma(pairs), one, dma(pairs), one, dma((n,)),
             ],
             compiler_params=pltpu.CompilerParams(
                 collective_id=0, has_side_effects=True, vmem_limit_bytes=VMEM_LIMIT),
@@ -694,11 +706,19 @@
                 jax.ShapeDtypeStruct((dim,), F32),
                 jax.ShapeDtypeStruct((heads,), F32),
             ),
-            in_specs=[any_spec] * 2 + [vmem] * 5,
-            out_specs=(any_spec,) * 2 + (vmem,) * 5,
+            in_specs=[any_spec] * 7,
+            out_specs=(any_spec,) * 7,
             scratch_shapes=[
                 pltpu.VMEM((2 * rows // TOK, TOK, dim), BF16),
-                dma((2 * rows // TOK,)), dma((2 * rows // TOK,)),
+                pltpu.VMEM((per_dev, 3 * dim), BF16),
+                pltpu.VMEM((per_dev, dim), BF16),
+                pltpu.VMEM((dim // LANES, LANES), F32),
+                pltpu.VMEM((dim // LANES, LANES), F32),
+                pltpu.VMEM((1, LANES), F32),
+                pltpu.VMEM((dim,), F32),
+                pltpu.VMEM((dim,), F32),
+                pltpu.VMEM((heads,), F32),
+                dma((2 * rows // TOK + 5,)), dma((2 * rows // TOK + 5,)),
             ],
             name="finish",
         )(*out)

time: 82.1 us -> 78.8 us (0.960)
  Pallas kernels: 81.2 us -> 77.9 us
    pallas_call x1, Pallas kernels: 73.8 us -> 71.9 us  [local_step(): pl.pallas_call(functools.partial(xca_kernel, n, heads), out_shape=(jax.Sh...]
    pallas_call x1, Pallas kernels: 7.44 us -> 6.01 us  [local_step(): pl.pallas_call(functools.partial(finish_kernel, heads), out_shape=(jax.Sh...]
where the time goes in v4:
time: 78.8 us; the launch traced here: 78.7 us
  Pallas kernels  77.9 us (99%)
  between operations  0.8 us (1%)
    pallas_call x1, Pallas kernels, local_step(): pl.pallas_call(functools.partial(xca_kernel, n, heads), out_shape=(jax.Sh...  71.9 us
    pallas_call x1, Pallas kernels, local_step(): pl.pallas_call(functools.partial(finish_kernel, heads), out_shape=(jax.Sh...  6.01 us

profile of v4, /device:TPU:113, one launch (start us, length us, event | category | flops | bytes accessed | tf_op | source)
XLA Modules:
  0.0 78.7 jit_solution(7841502747267544850)
XLA Ops:
  0.6 71.9 %xca_block.1 = (bf16[2048,768]{1,0:T(8,128)(2,1)}, bf16[2048,768]{1,0:T(8,128)(2,1)}, bf16[96,2304]{1,0:T(8,128)(2,1)}, bf16[96,768]{1,0:T(8,128)(2,1)}, f32[6,1...) custom-call(bf16[2,1024,768]{2,1,0:T(8,128)(2,1)} %x_hbm.1, bf16[2,1024,768]{2,1,0:T(8,128)(2,1)} %dy_hbm.1, ...), custom_call_target="tpu_custom_call" | custom-call | tf_op jit(solution)/shard_map/xca_block/pallas_call | solution.py:638
  72.5 6.0 %finish.1 = (bf16[2,1024,768]{2,1,0:T(8,128)(2,1)}, bf16[2,1024,768]{2,1,0:T(8,128)(2,1)}, bf16[96,2304]{1,0:T(8,128)(2,1)}, bf16[96,768]{1,0:T(8,128)(2,1)}, f3...) custom-call(bf16[2048,768]{1,0:T(8,128)(2,1)} %get-tuple-element.14.y_hbm, bf16[2048,768]{1,0:T(8,128)(2,1)} %get-tuple-element.15.dx_hbm, ...), custom_call_target="tpu_custom_call" | custom-call | tf_op jit(solution)/shard_map/finish/pallas_call | solution.py:698

commit v5 on v4

--- a/solution.py
+++ b/solution.py
@@ -51,6 +51,7 @@
     cr, cl, co = (chip + 1) % chips, (chip + chips - 1) % chips, (chip + 2) % chips
 
     peers = range(1, n)
+    most = pl.ds(0, n - 1)
     far_first = sorted(peers, key=lambda k: abs(2 * k - n))
 
     def rcopy(src, dst, ss, rs, dev):
@@ -113,13 +114,18 @@
         lax.fori_loop(0, count // COLS, body, 0)
 
     other_chips = range(1, chips)
+    others = pl.ds(1, chips - 1)
 
     def pair_sum(out, mid, ss, rs, b):
         return rcopy(out.at[b, 1 - core], mid.at[b], ss.at[0], rs.at[b, 0], partner)
 
     def chip_copy(out, into, ss, rs, b, k):
         to = (chip + k) % chips
-        return rcopy(out.at[b, core, to], into.at[b, k], ss.at[1], rs.at[b, k], to * 2 + core)
+        return rcopy(out.at[b, core, to], into.at[b, k], ss.at[1], rs.at[b, 1], to * 2 + core)
+
+    def chips_in(into, ss, rs, b):
+        got = into.at[b, others]
+        rcopy(got, got, ss.at[1], rs.at[b, 1], partner).wait_recv()
 
     def scatter_state(out, mid, into, ss, rs, b):
         pair_sum(out, mid, ss, rs, b).wait_recv()
@@ -249,20 +255,18 @@
         return jnp.concatenate([a0, a1, z], axis=1)
 
     def owner_forward(b):
-        for k in other_chips:
-            chip_copy(gs_out, gs_in, gs_s, gs_r, b, k).wait_recv()
+        chips_in(gs_in, gs_s, gs_r, b)
         gs_sum[b] = state_total(gs_out, gs_in, gs_s, gs_r, b)
         p0 = attn_state(b, 0)[2]
         p1 = attn_state(b, 1)[2]
         a_all[b, me] = pair(p0, p1).astype(BF16)
         for k in far_first:
             dst = (me + k) % n
-            rcopy(a_all.at[b, me], a_all.at[b, me], a_s.at[0], a_r.at[b, k], dst).start()
+            rcopy(a_all.at[b, me], a_all.at[b, me], a_s.at[0], a_r.at[b, 0], dst).start()
 
     def owner_backward():
         for b in range(images):
-            for k in other_chips:
-                chip_copy(ds_out, ds_in, ds_s, ds_r, b, k).wait_recv()
+            chips_in(ds_in, ds_s, ds_r, b)
         sub = lax.broadcasted_iota(jnp.int32, (8, LANES), 0)
         lane = lax.broadcasted_iota(jnp.int32, (8, LANES), 1)
         for b in range(images):
@@ -284,28 +288,26 @@
             for ref, ss, rs in states:
                 for k in (4, 2, 6, 1):
                     dst = (me + k) % n if k > 1 else partner
-                    rcopy(ref.at[b, me], ref.at[b, me], ss.at[0], rs.at[b, k], dst).start()
+                    rcopy(ref.at[b, me], ref.at[b, me], ss.at[0], rs.at[b, 1 if k == 1 else 0], dst).start()
 
     states = ((g_all, g_s, g_r), (c_all, c_s, c_r))
 
     def pass_on(b):
         for ref, ss, rs in states:
+            got = ref.at[b, pl.ds(0, chips - 1)]
+            rcopy(got, got, ss.at[0], rs.at[b, 0], partner).wait_recv()
             for k in (2, 6, 4):
                 src = (me + n - k) % n
-                rcopy(ref.at[b, me], ref.at[b, src], ss.at[0], rs.at[b, k], me).wait_recv()
-                rcopy(ref.at[b, src], ref.at[b, src], ss.at[0], rs.at[b, k + 1], partner).start()
+                rcopy(ref.at[b, src], ref.at[b, src], ss.at[0], rs.at[b, 1], partner).start()
 
     def passed(b):
         for ref, ss, rs in states:
-            rcopy(ref.at[b, me], ref.at[b, partner], ss.at[0], rs.at[b, 1], me).wait_recv()
-            for k in (2, 6, 4):
-                src = (partner + n - k) % n
-                rcopy(ref.at[b, me], ref.at[b, src], ss.at[0], rs.at[b, k + 1], me).wait_recv()
+            got = ref.at[b, pl.ds(0, chips)]
+            rcopy(got, got, ss.at[0], rs.at[b, 1], partner).wait_recv()
 
     def gathered(ref, ss, rs, b):
-        for k in peers:
-            src = (me + n - k) % n
-            rcopy(ref.at[b, me], ref.at[b, src], ss.at[0], rs.at[b, k], me).wait_recv()
+        got = ref.at[b, most]
+        rcopy(got, got, ss.at[0], rs.at[b, 0], partner).wait_recv()
 
     def grad_heads(b):
         cp_dy(b).wait()
@@ -391,12 +393,12 @@
     half = per_dev // 2
 
     def hop1(c):
-        return (rcopy(r1.at[c, co, pl.ds(0, half)], r2.at[c, 0], p1_s.at[0], p1_r.at[c, 0], right),
-                rcopy(r1.at[c, co, pl.ds(half, half)], r2.at[c, 1], p1_s.at[0], p1_r.at[c, 1], left))
+        return (rcopy(r1.at[c, co, pl.ds(0, half)], r2.at[c, 0], p1_s.at[0], p1_r.at[c], right),
+                rcopy(r1.at[c, co, pl.ds(half, half)], r2.at[c, 1], p1_s.at[0], p1_r.at[c], left))
 
     def hop2(c):
-        return (rcopy(r1.at[c, cr], r3.at[c, 0], p2_s.at[0], p2_r.at[c, 0], right),
-                rcopy(r1.at[c, cl], r3.at[c, 1], p2_s.at[0], p2_r.at[c, 1], left))
+        return (rcopy(r1.at[c, cr], r3.at[c, 0], p2_s.at[0], p2_r.at[c], right),
+                rcopy(r1.at[c, cl], r3.at[c, 1], p2_s.at[0], p2_r.at[c], left))
 
     def serve1(c):
         d2d(c).wait_recv()
@@ -406,16 +408,14 @@
             h.start()
 
     def serve2(c):
-        for h in hop1(c):
-            h.wait_recv()
+        rcopy(r2.at[c], r2.at[c], p1_s.at[0], p1_r.at[c], partner).wait_recv()
         r1[c, cr, 0:half] += r2[c, 0]
         r1[c, cl, half:per_dev] += r2[c, 1]
         for h in hop2(c):
             h.start()
 
     def serve3(c):
-        for h in hop2(c):
-            h.wait_recv()
+        rcopy(r3.at[c], r3.at[c], p2_s.at[0], p2_r.at[c], partner).wait_recv()
         return (r1[c, chip] + r3[c, 0] + r3[c, 1]).astype(BF16)
 
     def wo_chunk(c):
@@ -529,7 +529,7 @@
     lax.fori_loop(1, images * tiles, dx_body, 0)
     gb_all[me] = jnp.concatenate([jnp.sum(dgb[i], axis=0).reshape(dim // LANES, LANES) for i in range(2)], axis=0)
     for k in far_first:
-        rcopy(gb_all.at[me], gb_all.at[me], gb_s.at[0], gb_r.at[k], (me + k) % n).start()
+        rcopy(gb_all.at[me], gb_all.at[me], gb_s.at[0], gb_r.at[0], (me + k) % n).start()
 
     lane = lax.broadcasted_iota(jnp.int32, (1, LANES), 1)
     dtau = jnp.zeros((1, LANES), F32)
@@ -556,9 +556,8 @@
     finish_chunks(0, o_chunks, dwo_ref, dwo_hbm, 0, 0)
     finish_chunks(o_chunks, 2 * o_chunks, dwqkv_ref, dwqkv_hbm, v0, 1)
 
-    for k in peers:
-        src = (me + n - k) % n
-        rcopy(gb_all.at[me], gb_all.at[src], gb_s.at[0], gb_r.at[k], me).wait_recv()
+    got = gb_all.at[most]
+    rcopy(got, got, gb_s.at[0], gb_r.at[0], partner).wait_recv()
     tot = gb_all[0]
     for d in peers:
         tot = tot + gb_all[d]
@@ -571,10 +570,10 @@
     finish_chunks(2 * o_chunks, chunks, dwqkv_ref, dwqkv_hbm, -2 * o_chunks * COLS, 1)
 
     sent = (
-        (gs_mid, gs_s, 0), (gs_in.at[:, pl.ds(1, chips - 1)], gs_s, 1),
-        (ds_mid, ds_s, 0), (ds_in.at[:, pl.ds(1, chips - 1)], ds_s, 1),
-        (a_all.at[:, pl.ds(0, n - 1)], a_s, 0), (g_all.at[:, pl.ds(0, n - 1)], g_s, 0), (c_all.at[:, pl.ds(0, n - 1)], c_s, 0),
-        (gb_all.at[pl.ds(0, n - 1)], gb_s, 0), (r1, d2d_s, 0), (r2, p1_s, 0), (r3, p2_s, 0))
+        (gs_mid, gs_s, 0), (gs_in.at[:, others], gs_s, 1),
+        (ds_mid, ds_s, 0), (ds_in.at[:, others], ds_s, 1),
+        (a_all.at[:, most], a_s, 0), (g_all.at[:, most], g_s, 0), (c_all.at[:, most], c_s, 0),
+        (gb_all.at[most], gb_s, 0), (r1, d2d_s, 0), (r2, p1_s, 0), (r3, p2_s, 0))
     for ref, sem, i in sent:
         rcopy(ref, ref, sem.at[i], gb_r.at[0], partner).wait_send()
     pltpu.make_async_copy(x_v, y_hbm, out_sem.at[0]).wait()
@@ -633,8 +632,7 @@
         nwin = -(-heads // (COLS // hd))
         any_spec = pl.BlockSpec(memory_space=pl.ANY)
         dma = pltpu.SemaphoreType.DMA
-        pairs = (images, n)
-        one, by_chip = dma((1,)), dma((images, n // 2))
+        one, pairs = dma((1,)), dma((images, 2))
         out = pl.pallas_call(
             functools.partial(xca_kernel, n, heads),
             out_shape=(
@@ -687,9 +685,9 @@
                 pltpu.VMEM((chunks, 2, per_dev // 2, COLS), F32),
                 pltpu.VMEM((chunks, 2, per_dev, COLS), F32),
                 dma((rows // TOK + images + 7,)), dma((2,)), dma((5,)),
-                one, dma((chunks,)), one, dma((chunks, 2)), one, dma((chunks, 2)),
-                dma((2,)), by_chip, one, dma(pairs), dma((2,)), by_chip,
-                one, dma(pairs), one, dma(pairs), one, dma((n,)),
+                one, dma((chunks,)), one, dma((chunks,)), one, dma((chunks,)),
+                dma((2,)), pairs, one, pairs, dma((2,)), pairs,
+                one, pairs, one, pairs, one, one,
             ],
             compiler_params=pltpu.CompilerParams(
                 collective_id=0, has_side_effects=True, vmem_limit_bytes=VMEM_LIMIT),

time: 78.8 us -> 78.1 us (level)
  no operation moved by 1% of the time
where the time goes in v5:
time: 78.1 us; the launch traced here: 78 us
  Pallas kernels  77.2 us (99%)
  between operations  0.8 us (1%)
    pallas_call x1, Pallas kernels, local_step(): pl.pallas_call(functools.partial(xca_kernel, n, heads), out_shape=(jax.Sh...  71.2 us
    pallas_call x1, Pallas kernels, local_step(): pl.pallas_call(functools.partial(finish_kernel, heads), out_shape=(jax.Sh...  6.01 us

profile of v5, /device:TPU:113, one launch (start us, length us, event | category | flops | bytes accessed | tf_op | source)
XLA Modules:
  0.0 78.0 jit_solution(12123747410702081112)
XLA Ops:
  0.6 71.2 %xca_block.1 = (bf16[2048,768]{1,0:T(8,128)(2,1)}, bf16[2048,768]{1,0:T(8,128)(2,1)}, bf16[96,2304]{1,0:T(8,128)(2,1)}, bf16[96,768]{1,0:T(8,128)(2,1)}, f32[6,1...) custom-call(bf16[2,1024,768]{2,1,0:T(8,128)(2,1)} %x_hbm.1, bf16[2,1024,768]{2,1,0:T(8,128)(2,1)} %dy_hbm.1, ...), custom_call_target="tpu_custom_call" | custom-call | tf_op jit(solution)/shard_map/xca_block/pallas_call | solution.py:636
  71.8 6.0 %finish.1 = (bf16[2,1024,768]{2,1,0:T(8,128)(2,1)}, bf16[2,1024,768]{2,1,0:T(8,128)(2,1)}, bf16[96,2304]{1,0:T(8,128)(2,1)}, bf16[96,768]{1,0:T(8,128)(2,1)}, f3...) custom-call(bf16[2048,768]{1,0:T(8,128)(2,1)} %get-tuple-element.14.y_hbm, bf16[2048,768]{1,0:T(8,128)(2,1)} %get-tuple-element.15.dx_hbm, ...), custom_call_target="tpu_custom_call" | custom-call | tf_op jit(solution)/shard_map/finish/pallas_call | solution.py:696
